TPU v7x, 256 devices: a whole 4x4x8 slice. The times are simulated.
256 devices in a mesh: gx: 8 (over y, core), gy: 32 (over z, x).
Axes of the slice: x: 4, y: 4, z: 8, core: 2. Of those that a mesh axis runs over, the one named last changes fastest.
Arguments:
- offsets: float32 [2, 16, 256, 128], P(None, 'gx', 'gy'), may hold values from 0 to 1
- masses: float32 [16, 256, 128], P('gx', 'gy'), may hold values from 0.01 to 0.04
- counts: int32 [16, 256], P('gx', 'gy'), may hold values from 1 to 128, as said below
- source: float32 [16, 256, 128], P('gx', 'gy'), may hold values from -6 to 6
Outputs:
- density: float32 [16, 256, 128], P('gx', 'gy')
- pressure: float32 [16, 256, 128], P('gx', 'gy')
- residual: float32 [16, 256, 128], P('gx', 'gy')
- peaks: float32 [5], replicated
Inputs may be any that keep to these rules, and one draw needn't show every extreme that they name: `counts`: each cell's occupied slots come first; some cell holds 128 particles.
All inputs are finite; a program needn't handle non-finite values.
Results may differ from a plain program's by a relative error of at most 0.0003.
Values sent between devices are 32-bit elements; how exact they have to be, the bound alone decides.
A program may use at most 64 MiB of HBM per device.

v0:
```python
import jax
import jax.numpy as jnp
from jax import lax
from jax.sharding import Mesh
from jax.sharding import PartitionSpec as P

ITERS = 5
GX_GY = ("gx_0", "gx_1", "gy_0", "gy_1")
GX = ("gx_0", "gx_1")
GY = ("gy_0", "gy_1")


BASE_STIFF = 0.5
PAIR_SCALE = 0.05
NEIGHBOUR_STEPS = [(step_x, step_y) for step_x in (-1, 0, 1) for step_y in (-1, 0, 1)]


def extended(block, sides, width):
    for axis, dim in sides:
        count = lax.axis_size(axis)
        forward = [(i, i + 1) for i in range(count - 1)]
        backward = [(target, source) for source, target in forward]
        low = lax.ppermute(
            lax.slice_in_dim(block, block.shape[dim] - width, None, axis=dim), axis, forward
        )
        high = lax.ppermute(lax.slice_in_dim(block, 0, width, axis=dim), axis, backward)
        block = jnp.concatenate([low, block, high], axis=dim)
    return block


def one_axis_at_a_time(shard, axes):
    for axis in axes:
        shard = lax.psum(shard, axis)
    return shard


def merged_by_axis(shard, axes, combine):
    for axis in axes:
        pieces = jax.tree.map(lambda part: lax.all_gather(part, axis), shard)
        shard = jax.tree.map(lambda part: part[0], pieces)
        for k in range(1, lax.axis_size(axis)):
            shard = combine(shard, jax.tree.map(lambda part: part[k], pieces))
    return shard


def one_axis_at_a_time_2(shard, axes):
    for axis in axes:
        shard = lax.pmax(shard, axis)
    return shard


def near_view(padded, step_x, step_y):
    row_count = padded.shape[-3] - 2
    col_count = padded.shape[-2] - 2
    return padded[..., 1 + step_x : 1 + step_x + row_count, 1 + step_y : 1 + step_y + col_count, :]


def kernel_terms(own_cells, nearby, step_x, step_y):
    offset_x = step_x + nearby[0][..., None, :] - own_cells[0][..., :, None]
    offset_y = step_y + nearby[1][..., None, :] - own_cells[1][..., :, None]
    return jnp.maximum(1.0 - (offset_x * offset_x + offset_y * offset_y), 0.0)


def density_block(padded):
    own_cells = near_view(padded, 0, 0)
    summed = jnp.zeros(own_cells.shape[1:], jnp.float32)
    for step_x, step_y in NEIGHBOUR_STEPS:
        nearby = near_view(padded, step_x, step_y)
        falloff = kernel_terms(own_cells, nearby, step_x, step_y)
        summed = summed + jnp.sum(falloff * falloff * falloff * nearby[2][..., None, :], axis=-1)
    return 1.0 + summed


def pair_weights(padded, step_x, step_y):
    own_cells = near_view(padded, 0, 0)
    nearby = near_view(padded, step_x, step_y)
    falloff = kernel_terms(own_cells, nearby, step_x, step_y)
    pairing = (
        own_cells[3][..., :, None]
        * nearby[3][..., None, :]
        * (2.0 * PAIR_SCALE)
        / (own_cells[4][..., :, None] + nearby[4][..., None, :])
    )
    return falloff * falloff * pairing


def ghost_layer(fields):
    return extended(fields, ((GX, 1), (GY, 2)), 1)


def combine_three(earlier, later):
    return (earlier[0] + later[0], earlier[1] + later[1], jnp.maximum(earlier[2], later[2]))


def body(offsets, masses, counts, source):
    slot_count = offsets.shape[-1]
    occupied = (jnp.arange(slot_count, dtype=jnp.int32)[None, None, :] < counts[:, :, None]).astype(
        jnp.float32
    )
    fields = jnp.stack([offsets[0], offsets[1], masses * occupied, occupied])
    padded = ghost_layer(fields)
    density = density_block(padded)
    full = jnp.concatenate([padded, ghost_layer(density[None])], 0)
    summed = jnp.zeros(density.shape, jnp.float32)
    for step_x, step_y in NEIGHBOUR_STEPS:
        summed = summed + jnp.sum(pair_weights(full, step_x, step_y), axis=-1)
    diagonal = BASE_STIFF + summed

    def operate(vector):
        padded_field = ghost_layer(vector[None])[0]
        sums = jnp.zeros(vector.shape, jnp.float32)
        for step_x, step_y in NEIGHBOUR_STEPS:
            sums = sums + jnp.einsum(
                "xyij,xyj->xyi",
                pair_weights(full, step_x, step_y),
                near_view(padded_field, step_x, step_y),
                precision=lax.Precision.HIGHEST,
            )
        return diagonal * vector - sums

    pressure = jnp.zeros_like(source)
    residual = source * occupied
    scaled = residual / diagonal
    peak_list = []
    image = operate(scaled)
    precond_now, curvature_sum = (
        one_axis_at_a_time(jnp.sum(residual * scaled), GX_GY),
        one_axis_at_a_time(jnp.sum(scaled * image), GX_GY),
    )
    step_size = precond_now / curvature_sum
    direction = scaled
    along = image
    for step in range(ITERS):
        pressure = pressure + step_size * direction
        residual = residual - step_size * along
        if step + 1 < ITERS:
            scaled = residual / diagonal
            image = operate(scaled)
            precond_next, curvature_sum, peak_value = merged_by_axis(
                (jnp.sum(residual * scaled), jnp.sum(scaled * image), jnp.max(jnp.abs(residual))),
                GX_GY,
                combine_three,
            )
            ratio = precond_next / precond_now
            step_size = precond_next / (curvature_sum - ratio * precond_next / step_size)
            direction = scaled + ratio * direction
            along = image + ratio * along
            precond_now = precond_next
        else:
            peak_value = one_axis_at_a_time_2(jnp.max(jnp.abs(residual)), GX_GY)
        peak_list.append(peak_value)
    return (density, pressure, residual, jnp.stack(peak_list))


def solution(mesh):
    split = Mesh(mesh.devices.reshape(4, 2, 8, 4), ("gx_0", "gx_1", "gy_0", "gy_1"))
    return jax.shard_map(
        body,
        mesh=split,
        in_specs=(P(None, GX, GY, None), P(GX, GY, None), P(GX, GY), P(GX, GY, None)),
        out_specs=(P(GX, GY, None), P(GX, GY, None), P(GX, GY, None), P()),
        check_vma=False,
    )
```

profile of v0, /device:TPU:8, one launch (start us, length us, event | category | flops | bytes accessed | tf_op | source)
XLA Modules:
  0.0 612.5 jit_solution(141378854329659918)
XLA Ops:
  3.5 3.6 collective-permute-start.1
  9.9 4.5 collective-permute-start.2
  17.7 3.5 fusion.3
  29.5 4.8 collective-permute-start.6
  37.8 3.4 fusion.35
  41.2 3.4 fusion.29
  52.2 4.2 collective-permute-start.10
  57.7 4.2 collective-permute-done.11
  61.9 3.2 fusion.34
  65.1 3.2 fusion.28
  68.3 3.2 fusion.40
  71.5 3.2 fusion.46
  74.7 3.2 fusion.22
  77.9 3.2 fusion.52
  81.2 3.2 fusion.58
  84.4 3.2 fusion.64
  87.6 3.2 fusion.70
  91.5 9.3 %all-reduce.62 = (f32[]{:T(128)}, f32[]{:T(128)}) all-reduce(f32[]{:T(128)} %get-tuple-element.35, f32[]{:T(128)} %get-tuple-element.34), channel_id=1, replica_groups=mesh['gx_0'=4,'gx_1'=2,'gy_0'=8,'gy_1'=4] {'gx_0'}, use_global_device_ids=true, to_apply=%region_19.0 | all-reduce | flops 2 | bytes 16 | tf_op jit(solution)/shard_map/psum | solution.py:33
  103.9 27.9 %all-reduce.52 = (f32[]{:T(128)}, f32[]{:T(128)}) all-reduce(f32[]{:T(128)} %get-tuple-element.90, f32[]{:T(128)} %get-tuple-element.91), channel_id=1, replica_groups=mesh['gx_0'=4,'gx_1'=2,'gy_0'=8,'gy_1'=4] {'gy_0'}, use_global_device_ids=true, to_apply=%region_21.0 | all-reduce | flops 2 | bytes 16 | tf_op jit(solution)/shard_map/psum | solution.py:33
  131.7 13.8 %all-reduce.57 = (f32[]{:T(128)}, f32[]{:T(128)}) all-reduce(f32[]{:T(128)} %get-tuple-element.48, f32[]{:T(128)} %get-tuple-element.49), channel_id=1, replica_groups=mesh['gx_0'=4,'gx_1'=2,'gy_0'=8,'gy_1'=4] {'gy_1'}, use_global_device_ids=true, to_apply=%region_22.0 | all-reduce | flops 2 | bytes 16 | tf_op jit(solution)/shard_map/psum | solution.py:33
  148.9 3.6 collective-permute-start.13
  160.6 3.2 fusion.33
  163.8 3.2 fusion.27
  167.1 3.2 fusion.39
  170.3 3.2 fusion.45
  173.5 3.2 fusion.21
  176.7 3.2 fusion.51
  179.9 3.2 fusion.57
  183.1 3.2 fusion.63
  186.3 3.2 fusion.69
  193.6 8.4 %all-reduce.61 = (f32[4]{0:T(128)S(1)}, f32[4]{0:T(128)S(1)}) all-reduce(f32[4]{0:T(128)S(1)} %dynamic-update-slice, f32[4]{0:T(128)S(1)} %dynamic-update-slice.4), channel_id=1, replica_groups=mesh['gx_0'=4,'gx_1'=2,'gy_0'=8,'gy_1'=4] {'gx_0'}, use_global_device_ids=true, to_apply=%add | all-reduce | flops 8 | bytes 64
  208.9 18.1 %all-reduce.51 = (f32[8]{0:T(128)S(1)}, f32[8]{0:T(128)S(1)}) all-reduce(f32[8]{0:T(128)S(1)} %add_dynamic-update-slice_fusion.22, f32[8]{0:T(128)S(1)} %add_dynamic-update-slice_fusion.20), channel_id=1, replica_groups=mesh['gx_0'=4,'gx_1'=2,'gy_0'=8,'gy_1'=4] {'gy_0'}, use_global_device_ids=true, to_apply=%add.2 | all-reduce | flops 16 | bytes 128
  228.4 13.6 %all-reduce.56 = (f32[4]{0:T(128)S(1)}, f32[4]{0:T(128)S(1)}) all-reduce(f32[4]{0:T(128)S(1)} %add_dynamic-update-slice_fusion.7, f32[4]{0:T(128)S(1)} %add_dynamic-update-slice_fusion.6), channel_id=1, replica_groups=mesh['gx_0'=4,'gx_1'=2,'gy_0'=8,'gy_1'=4] {'gy_1'}, use_global_device_ids=true, to_apply=%add.3 | all-reduce | flops 8 | bytes 64
  251.7 3.6 collective-permute-start.17
  259.5 3.9 collective-permute-done.19
  263.5 3.2 fusion.32
  266.7 3.2 fusion.26
  269.9 3.2 fusion.38
  273.1 3.2 fusion.44
  282.7 3.2 fusion.56
  295.8 7.4 %all-reduce.60 = (f32[4]{0:T(128)S(1)}, f32[4]{0:T(128)S(1)}) all-reduce(f32[4]{0:T(128)S(1)} %dynamic-update-slice.8, f32[4]{0:T(128)S(1)} %dynamic-update-slice.12), channel_id=1, replica_groups=mesh['gx_0'=4,'gx_1'=2,'gy_0'=8,'gy_1'=4] {'gx_0'}, use_global_device_ids=true, to_apply=%add.8 | all-reduce | flops 8 | bytes 64
  308.9 17.8 %all-reduce.50 = (f32[8]{0:T(128)S(1)}, f32[8]{0:T(128)S(1)}) all-reduce(f32[8]{0:T(128)S(1)} %add_dynamic-update-slice_fusion.18, f32[8]{0:T(128)S(1)} %add_dynamic-update-slice_fusion.16), channel_id=1, replica_groups=mesh['gx_0'=4,'gx_1'=2,'gy_0'=8,'gy_1'=4] {'gy_0'}, use_global_device_ids=true, to_apply=%add.10 | all-reduce | flops 16 | bytes 128
  328.2 13.9 %all-reduce.55 = (f32[4]{0:T(128)S(1)}, f32[4]{0:T(128)S(1)}) all-reduce(f32[4]{0:T(128)S(1)} %add_dynamic-update-slice_fusion.5, f32[4]{0:T(128)S(1)} %add_dynamic-update-slice_fusion.4), channel_id=1, replica_groups=mesh['gx_0'=4,'gx_1'=2,'gy_0'=8,'gy_1'=4] {'gy_1'}, use_global_device_ids=true, to_apply=%add.11 | all-reduce | flops 8 | bytes 64
  350.4 3.6 collective-permute-start.21
  358.4 3.7 collective-permute-done.23
  362.2 3.2 fusion.31
  368.6 3.2 fusion.37
  378.2 3.2 fusion.49
  384.6 3.2 fusion.61
  394.5 8.2 %all-reduce.59 = (f32[4]{0:T(128)S(1)}, f32[4]{0:T(128)S(1)}) all-reduce(f32[4]{0:T(128)S(1)} %dynamic-update-slice.16, f32[4]{0:T(128)S(1)} %dynamic-update-slice.20), channel_id=1, replica_groups=mesh['gx_0'=4,'gx_1'=2,'gy_0'=8,'gy_1'=4] {'gx_0'}, use_global_device_ids=true, to_apply=%add.16 | all-reduce | flops 8 | bytes 64
  408.3 17.8 %all-reduce.49 = (f32[8]{0:T(128)S(1)}, f32[8]{0:T(128)S(1)}) all-reduce(f32[8]{0:T(128)S(1)} %add_dynamic-update-slice_fusion.14, f32[8]{0:T(128)S(1)} %add_dynamic-update-slice_fusion.12), channel_id=1, replica_groups=mesh['gx_0'=4,'gx_1'=2,'gy_0'=8,'gy_1'=4] {'gy_0'}, use_global_device_ids=true, to_apply=%add.18 | all-reduce | flops 16 | bytes 128
  427.6 13.9 %all-reduce.54 = (f32[4]{0:T(128)S(1)}, f32[4]{0:T(128)S(1)}) all-reduce(f32[4]{0:T(128)S(1)} %add_dynamic-update-slice_fusion.3, f32[4]{0:T(128)S(1)} %add_dynamic-update-slice_fusion.2), channel_id=1, replica_groups=mesh['gx_0'=4,'gx_1'=2,'gy_0'=8,'gy_1'=4] {'gy_1'}, use_global_device_ids=true, to_apply=%add.19 | all-reduce | flops 8 | bytes 64
  449.7 3.6 collective-permute-start.25
  461.8 3.2 fusion.30
  465.0 3.2 fusion.24
  468.2 3.2 fusion.36
  481.1 3.2 fusion.54
  487.5 3.2 fusion.66
  495.7 7.5 %all-reduce.58 = (f32[4]{0:T(128)S(1)}, f32[4]{0:T(128)S(1)}, f32[4]{0:T(128)S(1)}, f32[4]{0:T(128)S(1)}, f32[4]{0:T(128)S(1)}, /*index=5*/f32[4]{0:T(128)S(1)}) all-reduce(f32[4]{0:T(128)S(1)} %dynamic-update-slice.24, f32[4]{0:T(128)S(1)} %dynamic-update-slice.28, ...), channel_id=1, replica_groups=mesh['gx_0'=4,'gx_1'=2,'gy_0'=8,'gy_1'=4] {'gx_0'}, use_global_device_ids=true, to_apply=%add.24 | all-reduce | flops 24 | bytes 192
  515.2 20.7 %all-reduce.48 = (f32[8]{0:T(128)S(1)}, f32[8]{0:T(128)S(1)}, f32[8]{0:T(128)S(1)}, f32[8]{0:T(128)S(1)}, f32[8]{0:T(128)S(1)}, /*index=5*/f32[8]{0:T(128)S(1)}) all-reduce(f32[8]{0:T(128)S(1)} %add_dynamic-update-slice_fusion.10, f32[8]{0:T(128)S(1)} %add_dynamic-update-slice_fusion.8, ...), channel_id=1, replica_groups=mesh['gx_0'=4,'gx_1'=2,'gy_0'=8,'gy_1'=4] {'gy_0'}, use_global_device_ids=true, to_apply=%add.26 | all-reduce | flops 48 | bytes 384
  540.3 10.7 %all-reduce.53 = (f32[4]{0:T(128)S(1)}, f32[4]{0:T(128)S(1)}, f32[4]{0:T(128)S(1)}, f32[4]{0:T(128)S(1)}, f32[4]{0:T(128)S(1)}, /*index=5*/f32[4]{0:T(128)S(1)}) all-reduce(f32[4]{0:T(128)S(1)} %add_dynamic-update-slice_fusion.1, f32[4]{0:T(128)S(1)} %add_dynamic-update-slice_fusion, ...), channel_id=1, replica_groups=mesh['gx_0'=4,'gx_1'=2,'gy_0'=8,'gy_1'=4] {'gy_1'}, use_global_device_ids=true, to_apply=%add.27 | all-reduce | flops 24 | bytes 192
  560.6 10.6 %pmax.28 = f32[]{:T(128)} all-reduce(f32[]{:T(128)} %get-tuple-element.92), channel_id=1, replica_groups=mesh['gx_0'=4,'gx_1'=2,'gy_0'=8,'gy_1'=4] {'gx_0'}, use_global_device_ids=true, to_apply=%region_41.0 | all-reduce | flops 1 | bytes 8 | tf_op jit(solution)/shard_map/pmax | solution.py:48
  575.6 15.1 %pmax.30 = f32[]{:T(128)} all-reduce(f32[]{:T(128)} %pmax.29), channel_id=1, replica_groups=mesh['gx_0'=4,'gx_1'=2,'gy_0'=8,'gy_1'=4] {'gy_0'}, use_global_device_ids=true, to_apply=%region_43.0 | all-reduce | flops 1 | bytes 8 | tf_op jit(solution)/shard_map/pmax | solution.py:48
  590.7 10.4 %pmax.31 = f32[1]{0:T(128)} all-reduce(f32[1]{0:T(128)} %bitcast.258), channel_id=1, replica_groups=mesh['gx_0'=4,'gx_1'=2,'gy_0'=8,'gy_1'=4] {'gy_1'}, use_global_device_ids=true, to_apply=%region_44.0 | all-reduce | flops 1 | bytes 8 | tf_op jit(solution)/shard_map/pmax | solution.py:48
  (250 shorter events, 175.7 us)
Async XLA Ops:
  0.6 0.8 copy-start.3
  0.6 0.8 copy-start.4
  0.7 0.9 copy-start
  1.6 5.7 collective-permute-start
  3.5 5.1 collective-permute-start.1
  8.6 7.2 %collective-permute-start.3 = (f32[4,4,1,128]{3,2,1,0:T(1,128)S(1)}, f32[4,4,1,128]{3,2,1,0:T(1,128)S(1)}, u32[]{:S(2)}, u32[]{:S(2)}) collective-permute-start(f32[4,4,1,128]{3,2,1,0:T(1,128)S(1)} %get-tuple-element.135), channel_id=1, source_target_pairs={{1,0},{2,1},{3,2},{4,3},{5,4},{6,5},{7,6},{8,7},{9,8},{10,9},{11,1... | collective-permute-start | bytes 24584 | tf_op jit(solution)/shard_map/ppermute | solution.py:26
  9.9 5.9 collective-permute-start.2
  21.2 466.3 %copy-start.1 = (f32[2,8,128]{2,1,0:T(8,128)}, f32[2,8,128]{2,1,0:T(8,128)S(1)}, u32[]{:S(2)}) copy-start(f32[2,8,128]{2,1,0:T(8,128)S(1)} %add_add_fusion.1) | copy-start | bytes 24580
  21.2 5.6 collective-permute-start.4
  23.7 4.4 collective-permute-start.5
  28.1 6.2 %collective-permute-start.7 = (f32[1,4,1,128]{3,2,1,0:T(1,128)S(1)}, f32[1,4,1,128]{3,2,1,0:T(1,128)S(1)}, u32[]{:S(2)}, u32[]{:S(2)}) collective-permute-start(f32[1,4,1,128]{3,2,1,0:T(1,128)S(1)} %get-tuple-element.210), channel_id=1, source_target_pairs={{1,0},{2,1},{3,2},{4,3},{5,4},{6,5},{7,6},{8,7},{9,8},{10,9},{11,1... | collective-permute-start | bytes 6152 | tf_op jit(solution)/shard_map/ppermute | solution.py:26
  29.5 6.1 collective-permute-start.6
  44.5 0.7 copy-start.2
  45.3 5.6 collective-permute-start.8
  48.0 4.2 collective-permute-start.9
  52.2 5.5 collective-permute-start.10
  56.4 5.5 collective-permute-start.11
  146.9 5.6 collective-permute-start.12
  148.9 5.0 collective-permute-start.13
  153.8 4.2 collective-permute-start.14
  155.1 5.5 collective-permute-start.15
  156.6 0.7 copy-start.8
  191.5 1.4 copy-start.7
  202.8 0.8 copy-start.6
  207.5 0.8 copy-start.5
  249.8 5.6 collective-permute-start.16
  251.7 5.0 collective-permute-start.17
  256.7 2.8 collective-permute-start.18
  257.9 5.5 collective-permute-start.19
  348.5 5.6 collective-permute-start.20
  350.4 5.0 collective-permute-start.21
  355.4 3.1 collective-permute-start.22
  356.6 5.5 collective-permute-start.23
  447.8 5.6 collective-permute-start.24
  449.7 5.0 collective-permute-start.25
  454.7 7.1 %collective-permute-start.26 = (f32[1,4,1,128]{3,2,1,0:T(1,128)S(1)}, f32[1,4,1,128]{3,2,1,0:T(1,128)S(1)}, u32[]{:S(2)}, u32[]{:S(2)}) collective-permute-start(f32[1,4,1,128]{3,2,1,0:T(1,128)S(1)} %get-tuple-element.197), channel_id=1, source_target_pairs={{0,1},{1,2},{2,3},{3,4},{4,5},{5,6},{6,7},{7,8},{8,9},{9,10},{10,1... | collective-permute-start | bytes 6152 | tf_op jit(solution)/shard_map/ppermute | solution.py:23
  456.0 5.8 collective-permute-start.27
where the time goes:
time: 623 us; the launch traced here: 612 us
  blocking collectives  261 us (42%)
  matrix products  144 us (23%)
  starting transfers between devices  67.5 us (11%)
  other arithmetic  48.6 us (8%)
  between operations  35.4 us (6%)
  local copies, waits for them, and re-layouts  29.4 us (5%)
  waiting for transfers between devices  26.1 us (4%)
    unnamed x16, blocking collectives  168 us
    dot_general x45, matrix products, operate(): jnp.einsum('xyij,xyj->xyi', pair_weights(full, step_x, step_y), near_view...  144 us
    psum x4, blocking collectives, one_axis_at_a_time(): shard = lax.psum(shard, axis)  54.1 us
    pmax x4, blocking collectives, one_axis_at_a_time_2(): shard = lax.pmax(shard, axis)  39.2 us
    ppermute x14, starting transfers between devices, extended(): lax.ppermute(lax.slice_in_dim(block, 0, width, axis=dim), axis, backward)  34.2 us
    ppermute x14, starting transfers between devices, extended(): lax.ppermute(lax.slice_in_dim(block, block.shape[dim] - width, None, axis...  33.4 us
    unnamed x36, other arithmetic  28 us
    ppermute x14, waiting for transfers between devices, extended(): lax.ppermute(lax.slice_in_dim(block, 0, width, axis=dim), axis, backward)  23.5 us
  transfers between devices with their start and end apart: 28, of which 13 were waited for; matrix products, arithmetic and copies ran while one was open for 1% of the time, Pallas kernels for 0%

commit v1 on v0

v1 whole, which is shorter than its diff:
```python
import functools

import jax
import jax.numpy as jnp
from jax import lax
from jax.experimental import pallas as pl
from jax.experimental.pallas import tpu as pltpu
from jax.sharding import PartitionSpec as P

MESH = pl.DeviceIdType.MESH
F32 = jnp.float32

ITERS = 5
SLOT = 128
ROWS = 16
COLS = 256
GX = 8
XLEN = 4
ZLEN = 8
PLANE = GX * XLEN
BASE_STIFF = 0.5
FAR = 1000.0
LOW, HIGH = -0.05, 0.85
MID, HALF = (LOW + HIGH) / 2, (HIGH - LOW) / 2
PAIRS = [(i, j) for i in range(ITERS) for j in range(i, ITERS)] + [(i, ITERS) for i in range(ITERS)]
LOOP = 4


def snake(q):
    z, x = lax.div(q, XLEN), lax.rem(q, XLEN)
    return z * XLEN + x + lax.rem(z, 2) * (XLEN - 1 - 2 * x)


def mirrored(g, a):
    return a + lax.rem(g, 2) * (GX - 1 - 2 * a)


def device_of(column):
    group, place = lax.div(column, GX), lax.rem(column, GX)
    return mirrored(group, place), snake(group)


def body(
    off_ref, mass_ref, cnt_ref, src_ref,
    dens_ref, pres_ref, resid_ref, peaks_ref,
    sbuf, inb, xcol, ycol, rcol, wts, part, rb, vb, rows_s, ub, gb,
    g1s, g1, g2s, g2, p1s, p1, p2s, p2, osb, ob,
    in_send, in_recv, rho_send, rho_recv, halo_send, halo_recv,
    red_send, red_recv, out_send, out_recv,
):
    a, q = lax.axis_index("gx"), lax.axis_index("gy")
    z, x = lax.div(q, XLEN), lax.rem(q, XLEN)
    group = snake(q)
    place = mirrored(group, a)
    column = group * GX + place
    has_left, has_right = column > 0, column < COLS - 1
    left = device_of(jnp.maximum(column - 1, 0))
    right = device_of(jnp.minimum(column + 1, COLS - 1))
    plane_index = a * XLEN + x

    inb[...] = jnp.zeros_like(inb)
    rb[...] = jnp.zeros_like(rb)
    vb[...] = jnp.zeros_like(vb)
    osb[...] = jnp.zeros_like(osb)

    barrier = pltpu.get_barrier_semaphore()

    def plane_mate(t):
        other = lax.rem(plane_index + t, PLANE)
        return lax.div(other, XLEN), z * XLEN + lax.rem(other, XLEN)

    def tower_mate(t):
        return a, lax.rem(z + t, ZLEN) * XLEN + x

    def greet(target):
        pl.semaphore_signal(barrier, inc=1, device_id=target, device_id_type=MESH)

    for t in range(1, PLANE):
        greet(plane_mate(t))
    for t in range(1, ZLEN):
        greet(tower_mate(t))
    low_edge = (lax.rem(column, PLANE) == 0) & has_left
    high_edge = (lax.rem(column, PLANE) == PLANE - 1) & has_right
    for edge, step in ((low_edge, -1), (high_edge, 1)):
        @pl.when(edge)
        def _(step=step):
            for k in range(GX):
                greet((k, group + step))

    lane = lax.broadcasted_iota(jnp.int32, (1, SLOT), 1)
    for r in range(2):
        for c in range(GX):
            occ = jnp.where(lane < cnt_ref[r, c], 1.0, 0.0).astype(F32)
            sbuf[c, r, 0:1, :] = off_ref[0, r, c : c + 1, :]
            sbuf[c, r, 1:2, :] = off_ref[1, r, c : c + 1, :]
            sbuf[c, r, 2:3, :] = mass_ref[r, c : c + 1, :] * occ
            sbuf[c, r, 3:4, :] = src_ref[r, c : c + 1, :] * occ

    low_block = (x == 0) & (q > 0)
    high_block = (x == XLEN - 1) & (q < COLS // GX - 1)
    awaited = PLANE - 1 + ZLEN - 1 + low_block.astype(jnp.int32) + high_block.astype(jnp.int32)
    pl.semaphore_wait(barrier, awaited)

    sends = []
    for c in range(GX):
        for d in (-1, 0, 1):
            target_column = q * GX + c + d
            wanted = jnp.logical_and(target_column >= 0, target_column < COLS)
            ta, tq = device_of(jnp.clip(target_column, 0, COLS - 1))
            wanted = jnp.logical_and(wanted, jnp.logical_or(ta != a, tq != q))
            copy = pltpu.make_async_remote_copy(
                src_ref=sbuf.at[c],
                dst_ref=inb.at[1 - d, pl.ds(1 + 2 * a, 2)],
                send_sem=in_send.at[len(sends)],
                recv_sem=in_recv.at[1 - d],
                device_id=(ta, tq),
                device_id_type=MESH,
            )
            pl.when(wanted)(copy.start)
            sends.append((wanted, copy))
    for d in (-1, 0, 1):
        own = column + d - q * GX
        inside = (own >= 0) & (own < GX)
        copy = pltpu.make_async_copy(
            sbuf.at[jnp.clip(own, 0, GX - 1)],
            inb.at[1 + d, pl.ds(1 + 2 * a, 2)],
            in_recv.at[1 + d],
        )
        pl.when(inside)(copy.start)

    def arrived(slot):
        view = inb.at[slot, pl.ds(1, ROWS)]
        pltpu.make_async_copy(view, view, in_recv.at[slot]).wait()

    def spread(row):
        return jnp.transpose(jnp.broadcast_to(row, (SLOT, SLOT)))

    def total_row(block):
        return jnp.sum(jnp.transpose(block), axis=0, keepdims=True)

    arrived(1)

    def columns(r, carry):
        xcol[r] = spread(inb[1, r + 1, 0:1, :])
        ycol[r] = spread(inb[1, r + 1, 1:2, :])
        rows_s[0, pl.ds(r, 1), :] = inb[1, r + 1, 2:3, :]
        rows_s[1, pl.ds(r, 1), :] = inb[1, r + 1, 3:4, :]
        return carry

    lax.fori_loop(0, ROWS, columns, 0, unroll=LOOP)
    pl.when(has_left)(lambda: arrived(0))
    pl.when(has_right)(lambda: arrived(2))

    near = [(dc, dr) for dc in (1, 0, 2) for dr in (0, 1, 2)]

    def falloffs(r, carry):
        rows = []
        for dc, dr in near:
            cell = inb[dc, r + dr]
            mass = cell[2:3, :]
            px = (dr - 1.0) + jnp.where(mass > 0.0, cell[0:1, :], FAR)
            py = (dc - 1.0) + cell[1:2, :]
            rows.append((px, py, mass))
        for h in range(0, SLOT, 64):
            xi, yi = xcol[r, h : h + 64, :], ycol[r, h : h + 64, :]
            acc = jnp.zeros((64, SLOT), F32)
            for k, (px, py, mass) in enumerate(rows):
                ox, oy = px - xi, py - yi
                fall = jnp.maximum(1.0 - (ox * ox + oy * oy), 0.0)
                square = fall * fall
                wts[r, k, h : h + 64, :] = square
                acc = acc + square * fall * mass
            part[r, h : h + 64, :] = acc
        return carry

    lax.fori_loop(0, ROWS, falloffs, 0)

    def density_rows(r, carry):
        rb[1, pl.ds(8 + r, 1), :] = 1.0 + total_row(part[r])
        return carry

    lax.fori_loop(0, ROWS, density_rows, 0, unroll=LOOP)

    def exchange(buf, send, recv):
        copies = []
        for k, (have, target, slot) in enumerate(((has_left, left, 2), (has_right, right, 0))):
            copy = pltpu.make_async_remote_copy(
                src_ref=buf.at[1, pl.ds(8, ROWS)],
                dst_ref=buf.at[slot, pl.ds(8, ROWS)],
                send_sem=send.at[k],
                recv_sem=recv.at[slot],
                device_id=target,
                device_id_type=MESH,
            )
            pl.when(have)(copy.start)
            copies.append((have, copy))

        def wait():
            for have, slot in ((has_left, 0), (has_right, 2)):
                view = buf.at[slot, pl.ds(8, ROWS)]
                pl.when(have)(pltpu.make_async_copy(view, view, recv.at[slot]).wait)

        return wait, copies

    wait_rho, rho_copies = exchange(rb, rho_send, rho_recv)
    sends += rho_copies

    def rho_columns(r, carry):
        rcol[r] = spread(10.0 * rb[1, pl.ds(8 + r, 1), :])
        return carry

    lax.fori_loop(0, ROWS, rho_columns, 0, unroll=LOOP)

    def weights(first, last):
        def run(r, carry):
            rows = [10.0 * rb[dc, pl.ds(7 + r + dr, 1), :] for dc, dr in near[first:last]]
            for h in range(0, SLOT, 64):
                ri = rcol[r, h : h + 64, :]
                acc = jnp.zeros((64, SLOT), F32) if first == 0 else part[r, h : h + 64, :]
                for k, row in enumerate(rows, first):
                    w = wts[r, k, h : h + 64, :] / (ri + row)
                    wts[r, k, h : h + 64, :] = w
                    acc = acc + w
                part[r, h : h + 64, :] = acc
            return carry

        lax.fori_loop(0, ROWS, run, 0)

    weights(0, 3)
    wait_rho()
    weights(3, 9)

    def diagonal_rows(r, carry):
        ub[pl.ds(r, 1), :] = BASE_STIFF + total_row(part[r])
        return carry

    lax.fori_loop(0, ROWS, diagonal_rows, 0, unroll=LOOP)

    occ = jnp.where(rows_s[0] > 0.0, 1.0, 0.0).astype(F32)
    diag = ub[...]
    dinv = occ / diag
    basis = [rows_s[1] * dinv]
    gram_rows = {}

    for k in range(ITERS):
        vb[k, 1, pl.ds(8, ROWS), :] = basis[k]
        wait_halo, halo_copies = exchange(vb.at[k], halo_send.at[k], halo_recv.at[k])
        sends += halo_copies

        def apply_own(r, carry):
            acc = wts[r, 0] * vb[k, 1, pl.ds(7 + r, 1), :]
            for m in (1, 2):
                acc = acc + wts[r, m] * vb[k, 1, pl.ds(7 + r + m, 1), :]
            part[r] = acc
            return carry

        lax.fori_loop(0, ROWS, apply_own, 0, unroll=2)
        scaled = basis[k] * diag
        for i in range(k + 1):
            gram_rows[i, k] = jnp.sum(basis[i] * scaled, axis=0, keepdims=True)
        wait_halo()

        def apply_rest(r, carry):
            acc = part[r]
            for m in range(3, 9):
                dc, dr = near[m]
                acc = acc + wts[r, m] * vb[k, dc, pl.ds(7 + r + dr, 1), :]
            ub[pl.ds(r, 1), :] = total_row(acc)
            return carry

        lax.fori_loop(0, ROWS, apply_rest, 0, unroll=LOOP)
        moved = ub[...] * dinv - MID * basis[k]
        if k == 0:
            basis.append(moved * (1.0 / HALF))
        else:
            basis.append(moved * (2.0 / HALF) - basis[k - 1])

    scaled = basis[ITERS] * diag
    for i in range(ITERS):
        gram_rows[i, ITERS] = jnp.sum(basis[i] * scaled, axis=0, keepdims=True)

    sub24 = lax.broadcasted_iota(jnp.int32, (24, SLOT), 0)
    lane24 = lax.broadcasted_iota(jnp.int32, (24, SLOT), 1)
    sub8 = lax.broadcasted_iota(jnp.int32, (8, SLOT), 0)
    lane8 = lax.broadcasted_iota(jnp.int32, (8, SLOT), 1)

    gb[...] = jnp.zeros_like(gb)
    for k, pair in enumerate(PAIRS):
        gb[k : k + 1, :] = gram_rows[pair]
    sums = jnp.sum(gb[...], axis=1, keepdims=True)
    gram_row = jnp.sum(jnp.where(sub24 == lane24, sums, 0.0), axis=0, keepdims=True)

    def gather(row, own, all_refs, mates, index, count, send_sem, recv_sem):
        own[0] = row
        copies = []
        for t in range(1, count):
            copy = pltpu.make_async_remote_copy(
                src_ref=own.at[0],
                dst_ref=all_refs.at[index],
                send_sem=send_sem,
                recv_sem=recv_sem,
                device_id=mates(t),
                device_id_type=MESH,
            )
            copy.start()
        all_refs[index] = row

        def wait():
            view = all_refs.at[pl.ds(0, count - 1)]
            pltpu.make_async_copy(view, view, recv_sem).wait()

        def wait_sent():
            view = all_refs.at[pl.ds(0, count - 1)]
            pltpu.make_async_copy(view, view, send_sem).wait()

        return wait, wait_sent

    wait_plane, sent_plane = gather(gram_row, g1s, g1, plane_mate, plane_index, PLANE, red_send.at[0], red_recv.at[0])
    wait_plane()
    wait_tower, sent_tower = gather(jnp.sum(g1[...], axis=0), g2s, g2, tower_mate, z, ZLEN, red_send.at[1], red_recv.at[1])
    wait_tower()
    total = jnp.sum(g2[...], axis=0)

    entries = jnp.broadcast_to(
        jnp.sum(jnp.where(sub24 == lane24, total, 0.0), axis=1, keepdims=True), (24, SLOT)
    )
    gram = {}
    for k, (i, j) in enumerate(PAIRS):
        gram[i, j] = gram[j, i] = entries[k : k + 1, :]

    def dot(left_side, right_side):
        out = None
        for i, u in enumerate(left_side):
            inner = None
            for j, v in enumerate(right_side):
                term = gram[i, j] * v
                inner = term if inner is None else inner + term
            out = u * inner if out is None else out + u * inner
        return out

    one = jnp.ones((1, SLOT), F32)
    zero = jnp.zeros((1, SLOT), F32)
    solution_at, residual_at, direction = [], [one], [one]
    residuals = []
    rz = gram[0, 0]
    for k in range(ITERS):
        image = [zero] * (k + 2)
        for j, u in enumerate(direction):
            image[j] = image[j] + (1.0 - MID) * u
            if j == 0:
                image[1] = image[1] - HALF * u
            else:
                image[j + 1] = image[j + 1] - (HALF / 2) * u
                image[j - 1] = image[j - 1] - (HALF / 2) * u
        step = rz / dot(direction, image)
        solution_at = [
            (solution_at[j] if j < len(solution_at) else zero) + step * u for j, u in enumerate(direction)
        ]
        residual_at = [
            (residual_at[j] if j < len(residual_at) else zero) - step * u for j, u in enumerate(image)
        ]
        residuals.append(residual_at)
        if k + 1 < ITERS:
            new = dot(residual_at, residual_at)
            ratio = new / rz
            direction = [
                u + (ratio * direction[j] if j < len(direction) else zero) for j, u in enumerate(residual_at)
            ]
            rz = new

    def combine(factors):
        out = None
        for u, v in zip(factors, basis):
            out = u * v if out is None else out + u * v
        return out

    pressure = combine(solution_at)
    gb[0:8, :] = jnp.zeros((8, SLOT), F32)
    for k in range(ITERS):
        field = combine(residuals[k]) * diag
        gb[k : k + 1, :] = jnp.max(jnp.abs(field), axis=0, keepdims=True)
    peak = jnp.max(gb[0:8, :], axis=1, keepdims=True)
    peak_row = jnp.sum(jnp.where(sub8 == lane8, peak, 0.0), axis=0, keepdims=True)
    wait_peaks, sent_peaks = gather(peak_row, p1s, p1, plane_mate, plane_index, PLANE, red_send.at[2], red_recv.at[2])

    density = rb[1, pl.ds(8, ROWS), :]
    for r in range(ROWS):
        osb[r, 0:1, :] = density[r : r + 1, :]
        osb[r, 1:2, :] = pressure[r : r + 1, :]
        osb[r, 2:3, :] = field[r : r + 1, :]
    for k in range(GX):
        wanted = jnp.logical_or(a != k, group != q)
        copy = pltpu.make_async_remote_copy(
            src_ref=osb.at[pl.ds(2 * k, 2)],
            dst_ref=ob.at[place],
            send_sem=out_send.at[k],
            recv_sem=out_recv,
            device_id=(k, group),
            device_id_type=MESH,
        )
        pl.when(wanted)(copy.start)
        sends.append((wanted, copy))
    local = pltpu.make_async_copy(osb.at[pl.ds(2 * a, 2)], ob.at[place], out_recv)
    pl.when(group == q)(local.start)

    wait_peaks()
    wait_top, sent_top = gather(jnp.max(p1[...], axis=0), p2s, p2, tower_mate, z, ZLEN, red_send.at[3], red_recv.at[3])
    pltpu.make_async_copy(ob, ob, out_recv).wait()
    for r in range(2):
        for c in range(GX):
            dens_ref[r, c : c + 1, :] = ob[c, r, 0:1, :]
            pres_ref[r, c : c + 1, :] = ob[c, r, 1:2, :]
            resid_ref[r, c : c + 1, :] = ob[c, r, 2:3, :]
    wait_top()
    peaks_ref[...] = jnp.max(p2[...], axis=0)

    for wanted, copy in sends:
        pl.when(wanted)(copy.wait_send)
    for wait in (sent_plane, sent_tower, sent_peaks, sent_top):
        wait()


def shard(offsets, masses, counts, source):
    block = jax.ShapeDtypeStruct((2, GX, SLOT), F32)
    vmem = pl.BlockSpec(memory_space=pltpu.VMEM)
    dma = pltpu.SemaphoreType.DMA
    cells = (ROWS, SLOT, SLOT)
    density, pressure, residual, peaks = pl.pallas_call(
        body,
        out_shape=(block, block, block, jax.ShapeDtypeStruct((1, SLOT), F32)),
        in_specs=[vmem, vmem, pl.BlockSpec(memory_space=pltpu.SMEM), vmem],
        out_specs=(vmem, vmem, vmem, vmem),
        scratch_shapes=[
            pltpu.VMEM((GX, 2, 4, SLOT), F32),
            pltpu.VMEM((3, ROWS + 2, 4, SLOT), F32),
            pltpu.VMEM(cells, F32),
            pltpu.VMEM(cells, F32),
            pltpu.VMEM(cells, F32),
            pltpu.VMEM((ROWS, 9, SLOT, SLOT), F32),
            pltpu.VMEM(cells, F32),
            pltpu.VMEM((3, 32, SLOT), F32),
            pltpu.VMEM((ITERS, 3, 32, SLOT), F32),
            pltpu.VMEM((2, ROWS, SLOT), F32),
            pltpu.VMEM((ROWS, SLOT), F32),
            pltpu.VMEM((24, SLOT), F32),
            pltpu.VMEM((1, 1, SLOT), F32),
            pltpu.VMEM((PLANE, 1, SLOT), F32),
            pltpu.VMEM((1, 1, SLOT), F32),
            pltpu.VMEM((ZLEN, 1, SLOT), F32),
            pltpu.VMEM((1, 1, SLOT), F32),
            pltpu.VMEM((PLANE, 1, SLOT), F32),
            pltpu.VMEM((1, 1, SLOT), F32),
            pltpu.VMEM((ZLEN, 1, SLOT), F32),
            pltpu.VMEM((ROWS, 4, SLOT), F32),
            pltpu.VMEM((GX, 2, 4, SLOT), F32),
            dma((24,)),
            dma((3,)),
            dma((2,)),
            dma((3,)),
            dma((ITERS, 2)),
            dma((ITERS, 3)),
            dma((4,)),
            dma((4,)),
            dma((GX,)),
            dma,
        ],
        compiler_params=pltpu.CompilerParams(collective_id=0, has_side_effects=True),
    )(offsets, masses, counts, source)
    return density, pressure, residual, peaks[0, :ITERS]


def solution(mesh):
    return jax.shard_map(
        shard,
        mesh=mesh,
        in_specs=(P(None, "gx", "gy", None), P("gx", "gy", None), P("gx", "gy"), P("gx", "gy", None)),
        out_specs=(P("gx", "gy", None), P("gx", "gy", None), P("gx", "gy", None), P()),
        check_vma=False,
    )
```

time: 623 us -> 69.2 us (0.11)
  the two profiles are of different devices: /device:TPU:8 before, /device:TPU:1 now
where the time goes in v1:
time: 69.2 us; the launch traced here: 68.9 us
  Pallas kernels  65 us (94%)
  local copies, waits for them, and re-layouts  3.2 us (5%)
    pallas_call x1, Pallas kernels, shard(): pl.pallas_call(body, out_shape=(block, block, block, jax.ShapeDtypeStruct...  65 us
    unnamed x9, local copies, waits for them, and re-layouts  2 us

profile of v1, /device:TPU:1, one launch (start us, length us, event | category | flops | bytes accessed | tf_op | source)
XLA Modules:
  0.0 68.9 jit_solution(5644327641159252022)
XLA Ops:
  0.6 65.0 %shard_map.75 = (f32[2,8,128]{2,1,0:T(8,128)}, f32[2,8,128]{2,1,0:T(8,128)}, f32[2,8,128]{2,1,0:T(8,128)}, f32[1,128]{1,0:T(1,128)}) custom-call(f32[2,2,8,128]{3,2,1,0:T(8,128)} %off_ref.1, f32[2,8,128]{2,1,0:T(8,128)} %mass_ref.1, s32[2,8]{1,0:T(2,128)} %cnt_ref.1, f32[2,8,128]{2,1,0:T(8,128)} %src_ref.1), custom_call_target="tpu_custom_call" | custom-call | tf_op jit(solution)/shard_map/pallas_call | solution.py:428
  65.7 0.0 copy-start.2
  65.7 1.2 %slice_bitcast_fusion = f32[5]{0:T(128)} fusion(f32[1,128]{1,0:T(1,128)} %get-tuple-element.11), kind=kLoop, calls=%fused_computation | loop fusion | bytes 40 | tf_op jit(solution)/shard_map/squeeze | solution.py:469
  66.9 0.0 copy-done.2
  66.9 0.0 copy-start.1
  66.9 0.6 copy.11
  67.5 0.1 copy-done.1
  67.6 0.0 copy-start
  67.6 0.6 copy.12
  68.2 0.1 copy-done
  68.3 0.6 copy.13
Async XLA Ops:
  65.7 1.2 %copy-start.2 = (f32[2,8,128]{2,1,0:T(8,128)S(1)}, f32[2,8,128]{2,1,0:T(8,128)}, u32[]{:S(2)}) copy-start(f32[2,8,128]{2,1,0:T(8,128)} %get-tuple-element.16) | copy-start | bytes 24580
  66.9 0.7 %copy-start.1 = (f32[2,8,128]{2,1,0:T(8,128)S(1)}, f32[2,8,128]{2,1,0:T(8,128)}, u32[]{:S(2)}) copy-start(f32[2,8,128]{2,1,0:T(8,128)} %get-tuple-element.17) | copy-start | bytes 24580
  67.6 0.7 %copy-start = (f32[2,8,128]{2,1,0:T(8,128)S(1)}, f32[2,8,128]{2,1,0:T(8,128)}, u32[]{:S(2)}) copy-start(f32[2,8,128]{2,1,0:T(8,128)} %get-tuple-element.18) | copy-start | bytes 24580

commit v2 on v1

--- a/solution.py
+++ b/solution.py
@@ -20,8 +20,7 @@
 PLANE = GX * XLEN
 BASE_STIFF = 0.5
 FAR = 1000.0
-LOW, HIGH = -0.05, 0.85
-MID, HALF = (LOW + HIGH) / 2, (HIGH - LOW) / 2
+SHIFTS = (0.8125, 0.0625, 0.8125, 0.125, 0.5)
 PAIRS = [(i, j) for i in range(ITERS) for j in range(i, ITERS)] + [(i, ITERS) for i in range(ITERS)]
 LOOP = 4
 
@@ -35,6 +34,68 @@
     return a + lax.rem(g, 2) * (GX - 1 - 2 * a)
 
 
+def two_sum(a, b):
+    s = a + b
+    t = s - a
+    return s, (a - (s - t)) + (b - t)
+
+
+def fast_two_sum(a, b):
+    s = a + b
+    return s, b - (s - a)
+
+
+def split(a):
+    c = 4097.0 * a
+    high = c - (c - a)
+    return high, a - high
+
+
+def two_prod(a, b):
+    p = a * b
+    ah, al = split(a)
+    bh, bl = split(b)
+    return p, ((ah * bh - p) + ah * bl + al * bh) + al * bl
+
+
+def pair_add(u, v):
+    s, e = two_sum(u[0], v[0])
+    return fast_two_sum(s, e + (u[1] + v[1]))
+
+
+def pair_neg(u):
+    return -u[0], -u[1]
+
+
+def pair_mul(u, v):
+    p, e = two_prod(u[0], v[0])
+    return fast_two_sum(p, e + (u[0] * v[1] + u[1] * v[0]))
+
+
+def pair_scale(u, c):
+    p, e = two_prod(u[0], c)
+    return fast_two_sum(p, e + u[1] * c)
+
+
+def pair_div(u, v):
+    q = u[0] / v[0]
+    r = pair_add(u, pair_neg(pair_scale(v, q)))
+    return fast_two_sum(q, r[0] / v[0])
+
+
+def pair_tree(items):
+    while len(items) > 1:
+        items = [pair_add(*items[k : k + 2]) if k + 1 < len(items) else items[k] for k in range(0, len(items), 2)]
+    return items[0]
+
+
+def pair_dot(u, v):
+    out = pair_mul(u, v)
+    for shift in (4, 2, 1):
+        out = pair_add(out, (pltpu.roll(out[0], shift, 0), pltpu.roll(out[1], shift, 0)))
+    return out
+
+
 def device_of(column):
     group, place = lax.div(column, GX), lax.rem(column, GX)
     return mirrored(group, place), snake(group)
@@ -42,9 +103,9 @@
 
 def body(
     off_ref, mass_ref, cnt_ref, src_ref,
-    dens_ref, pres_ref, resid_ref, peaks_ref,
+    ob, p2,
     sbuf, inb, xcol, ycol, rcol, wts, part, rb, vb, rows_s, ub, gb,
-    g1s, g1, g2s, g2, p1s, p1, p2s, p2, osb, ob,
+    g1s, g1, g2s, g2, p1s, p1, p2s, osb,
     in_send, in_recv, rho_send, rho_recv, halo_send, halo_recv,
     red_send, red_recv, out_send, out_recv,
 ):
@@ -62,6 +123,8 @@
     rb[...] = jnp.zeros_like(rb)
     vb[...] = jnp.zeros_like(vb)
     osb[...] = jnp.zeros_like(osb)
+    gb[...] = jnp.zeros_like(gb)
+    part[0] = jnp.zeros((SLOT, SLOT), F32)
 
     barrier = pltpu.get_barrier_semaphore()
 
@@ -147,13 +210,24 @@
         rows_s[1, pl.ds(r, 1), :] = inb[1, r + 1, 3:4, :]
         return carry
 
-    lax.fori_loop(0, ROWS, columns, 0, unroll=LOOP)
+    def columns(r):
+        xcol[r] = spread(inb[1, r + 1, 0:1, :])
+        ycol[r] = spread(inb[1, r + 1, 1:2, :])
+        rows_s[0, pl.ds(r, 1), :] = inb[1, r + 1, 2:3, :]
+        rows_s[1, pl.ds(r, 1), :] = inb[1, r + 1, 3:4, :]
+
+    columns(0)
     pl.when(has_left)(lambda: arrived(0))
     pl.when(has_right)(lambda: arrived(2))
 
     near = [(dc, dr) for dc in (1, 0, 2) for dr in (0, 1, 2)]
 
+    def density_row(r):
+        rb[1, pl.ds(8 + r, 1), :] = 1.0 + total_row(part[r])
+
     def falloffs(r, carry):
+        columns(jnp.minimum(r + 1, ROWS - 1))
+        density_row(jnp.maximum(r - 1, 0))
         rows = []
         for dc, dr in near:
             cell = inb[dc, r + dr]
@@ -174,12 +248,7 @@
         return carry
 
     lax.fori_loop(0, ROWS, falloffs, 0)
-
-    def density_rows(r, carry):
-        rb[1, pl.ds(8 + r, 1), :] = 1.0 + total_row(part[r])
-        return carry
-
-    lax.fori_loop(0, ROWS, density_rows, 0, unroll=LOOP)
+    density_row(ROWS - 1)
 
     def exchange(buf, send, recv):
         copies = []
@@ -209,10 +278,15 @@
         rcol[r] = spread(10.0 * rb[1, pl.ds(8 + r, 1), :])
         return carry
 
-    lax.fori_loop(0, ROWS, rho_columns, 0, unroll=LOOP)
+    lax.fori_loop(0, ROWS, rho_columns, 0, unroll=ROWS)
+
+    def diagonal_row(r):
+        ub[pl.ds(r, 1), :] = BASE_STIFF + total_row(part[r])
 
     def weights(first, last):
         def run(r, carry):
+            if first:
+                diagonal_row(jnp.maximum(r - 1, 0))
             rows = [10.0 * rb[dc, pl.ds(7 + r + dr, 1), :] for dc, dr in near[first:last]]
             for h in range(0, SLOT, 64):
                 ri = rcol[r, h : h + 64, :]
@@ -230,12 +304,7 @@
     wait_rho()
     weights(3, 9)
 
-    def diagonal_rows(r, carry):
-        ub[pl.ds(r, 1), :] = BASE_STIFF + total_row(part[r])
-        return carry
-
-    lax.fori_loop(0, ROWS, diagonal_rows, 0, unroll=LOOP)
-
+    diagonal_row(ROWS - 1)
     occ = jnp.where(rows_s[0] > 0.0, 1.0, 0.0).astype(F32)
     diag = ub[...]
     dinv = occ / diag
@@ -268,31 +337,28 @@
             ub[pl.ds(r, 1), :] = total_row(acc)
             return carry
 
-        lax.fori_loop(0, ROWS, apply_rest, 0, unroll=LOOP)
-        moved = ub[...] * dinv - MID * basis[k]
-        if k == 0:
-            basis.append(moved * (1.0 / HALF))
-        else:
-            basis.append(moved * (2.0 / HALF) - basis[k - 1])
+        lax.fori_loop(0, ROWS, apply_rest, 0, unroll=ROWS)
+        basis.append(2.0 * (ub[...] * dinv - SHIFTS[k] * basis[k]))
 
     scaled = basis[ITERS] * diag
     for i in range(ITERS):
         gram_rows[i, ITERS] = jnp.sum(basis[i] * scaled, axis=0, keepdims=True)
 
-    sub24 = lax.broadcasted_iota(jnp.int32, (24, SLOT), 0)
-    lane24 = lax.broadcasted_iota(jnp.int32, (24, SLOT), 1)
     sub8 = lax.broadcasted_iota(jnp.int32, (8, SLOT), 0)
     lane8 = lax.broadcasted_iota(jnp.int32, (8, SLOT), 1)
 
-    gb[...] = jnp.zeros_like(gb)
-    for k, pair in enumerate(PAIRS):
-        gb[k : k + 1, :] = gram_rows[pair]
-    sums = jnp.sum(gb[...], axis=1, keepdims=True)
-    gram_row = jnp.sum(jnp.where(sub24 == lane24, sums, 0.0), axis=0, keepdims=True)
-
-    def gather(row, own, all_refs, mates, index, count, send_sem, recv_sem):
-        own[0] = row
-        copies = []
+    for i, j in PAIRS:
+        gb[8 * j + i : 8 * j + i + 1, :] = gram_rows[i, j]
+        if i != j:
+            gb[8 * i + j : 8 * i + j + 1, :] = gram_rows[i, j]
+    turned = jnp.transpose(gb[...])
+    gram_sum = two_sum(turned[:64], turned[64:])
+    for size in (32, 16, 8, 4, 2, 1):
+        gram_sum = pair_add((gram_sum[0][:size], gram_sum[1][:size]), (gram_sum[0][size:], gram_sum[1][size:]))
+
+    def gather(rows, own, all_refs, mates, index, count, send_sem, recv_sem):
+        for k, row in enumerate(rows):
+            own[0, k : k + 1, :] = row
         for t in range(1, count):
             copy = pltpu.make_async_remote_copy(
                 src_ref=own.at[0],
@@ -303,7 +369,8 @@
                 device_id_type=MESH,
             )
             copy.start()
-        all_refs[index] = row
+        for k, row in enumerate(rows):
+            all_refs[index, k : k + 1, :] = row
 
         def wait():
             view = all_refs.at[pl.ds(0, count - 1)]
@@ -315,73 +382,60 @@
 
         return wait, wait_sent
 
-    wait_plane, sent_plane = gather(gram_row, g1s, g1, plane_mate, plane_index, PLANE, red_send.at[0], red_recv.at[0])
+    def pairs_of(refs, count):
+        return pair_tree([(refs[k, 0:1, :], refs[k, 1:2, :]) for k in range(count)])
+
+    wait_plane, sent_plane = gather(gram_sum, g1s, g1, plane_mate, plane_index, PLANE, red_send.at[0], red_recv.at[0])
     wait_plane()
-    wait_tower, sent_tower = gather(jnp.sum(g1[...], axis=0), g2s, g2, tower_mate, z, ZLEN, red_send.at[1], red_recv.at[1])
+    plane_sum = pairs_of(g1, PLANE)
+    wait_tower, sent_tower = gather(plane_sum, g2s, g2, tower_mate, z, ZLEN, red_send.at[1], red_recv.at[1])
     wait_tower()
-    total = jnp.sum(g2[...], axis=0)
-
-    entries = jnp.broadcast_to(
-        jnp.sum(jnp.where(sub24 == lane24, total, 0.0), axis=1, keepdims=True), (24, SLOT)
-    )
-    gram = {}
-    for k, (i, j) in enumerate(PAIRS):
-        gram[i, j] = gram[j, i] = entries[k : k + 1, :]
-
-    def dot(left_side, right_side):
+    total = pairs_of(g2, ZLEN)
+    high, low = spread(total[0]), spread(total[1])
+    gram = [(high[8 * j : 8 * j + 8], low[8 * j : 8 * j + 8]) for j in range(ITERS + 1)]
+
+    zero = jnp.zeros((8, SLOT), F32)
+    first = jnp.where(sub8 == 0, 1.0, 0.0).astype(F32)
+    keep = zero
+    for k, shift in enumerate(SHIFTS):
+        keep = jnp.where(sub8 == k, 1.0 - shift, keep)
+
+    def part_of(u, k):
+        return tuple(jnp.broadcast_to(w[k : k + 1], (8, SLOT)) for w in u)
+
+    solution_at, residual_at, direction = (zero, zero), (first, zero), (first, zero)
+    residual_image = gram[0]
+    residuals = []
+    rz = part_of(gram[0], 0)
+    for k in range(ITERS):
+        moved = tuple(-0.5 * pltpu.roll(w, 1, 0) for w in direction)
+        image = pair_add(pair_scale(direction, keep), moved)
+        gram_image = pair_tree([pair_mul(gram[j], part_of(image, j)) for j in range(k + 2)])
+        step = pair_div(rz, pair_dot(direction, gram_image))
+        solution_at = pair_add(solution_at, pair_mul(step, direction))
+        residual_at = pair_add(residual_at, pair_neg(pair_mul(step, image)))
+        residuals.append(residual_at[0])
+        if k + 1 < ITERS:
+            residual_image = pair_add(residual_image, pair_neg(pair_mul(step, gram_image)))
+            new = pair_dot(residual_at, residual_image)
+            direction = pair_add(residual_at, pair_mul(pair_div(new, rz), direction))
+            rz = new
+
+    def combine(factors, count):
         out = None
-        for i, u in enumerate(left_side):
-            inner = None
-            for j, v in enumerate(right_side):
-                term = gram[i, j] * v
-                inner = term if inner is None else inner + term
-            out = u * inner if out is None else out + u * inner
+        for j in range(count):
+            term = factors[j : j + 1] * basis[j]
+            out = term if out is None else out + term
         return out
 
-    one = jnp.ones((1, SLOT), F32)
-    zero = jnp.zeros((1, SLOT), F32)
-    solution_at, residual_at, direction = [], [one], [one]
-    residuals = []
-    rz = gram[0, 0]
-    for k in range(ITERS):
-        image = [zero] * (k + 2)
-        for j, u in enumerate(direction):
-            image[j] = image[j] + (1.0 - MID) * u
-            if j == 0:
-                image[1] = image[1] - HALF * u
-            else:
-                image[j + 1] = image[j + 1] - (HALF / 2) * u
-                image[j - 1] = image[j - 1] - (HALF / 2) * u
-        step = rz / dot(direction, image)
-        solution_at = [
-            (solution_at[j] if j < len(solution_at) else zero) + step * u for j, u in enumerate(direction)
-        ]
-        residual_at = [
-            (residual_at[j] if j < len(residual_at) else zero) - step * u for j, u in enumerate(image)
-        ]
-        residuals.append(residual_at)
-        if k + 1 < ITERS:
-            new = dot(residual_at, residual_at)
-            ratio = new / rz
-            direction = [
-                u + (ratio * direction[j] if j < len(direction) else zero) for j, u in enumerate(residual_at)
-            ]
-            rz = new
-
-    def combine(factors):
-        out = None
-        for u, v in zip(factors, basis):
-            out = u * v if out is None else out + u * v
-        return out
-
-    pressure = combine(solution_at)
+    pressure = combine(solution_at[0], ITERS)
     gb[0:8, :] = jnp.zeros((8, SLOT), F32)
     for k in range(ITERS):
-        field = combine(residuals[k]) * diag
+        field = combine(residuals[k], k + 2) * diag
         gb[k : k + 1, :] = jnp.max(jnp.abs(field), axis=0, keepdims=True)
     peak = jnp.max(gb[0:8, :], axis=1, keepdims=True)
     peak_row = jnp.sum(jnp.where(sub8 == lane8, peak, 0.0), axis=0, keepdims=True)
-    wait_peaks, sent_peaks = gather(peak_row, p1s, p1, plane_mate, plane_index, PLANE, red_send.at[2], red_recv.at[2])
+    wait_peaks, sent_peaks = gather([peak_row], p1s, p1, plane_mate, plane_index, PLANE, red_send.at[2], red_recv.at[2])
 
     density = rb[1, pl.ds(8, ROWS), :]
     for r in range(ROWS):
@@ -404,20 +458,23 @@
     pl.when(group == q)(local.start)
 
     wait_peaks()
-    wait_top, sent_top = gather(jnp.max(p1[...], axis=0), p2s, p2, tower_mate, z, ZLEN, red_send.at[3], red_recv.at[3])
+    wait_top, sent_top = gather([jnp.max(p1[...], axis=0)], p2s, p2, tower_mate, z, ZLEN, red_send.at[3], red_recv.at[3])
     pltpu.make_async_copy(ob, ob, out_recv).wait()
+    wait_top()
+
+    for wanted, copy in sends:
+        pl.when(wanted)(copy.wait_send)
+    for wait in (sent_plane, sent_tower, sent_peaks, sent_top):
+        wait()
+
+
+def finish(ob, p2, dens_ref, pres_ref, resid_ref, peaks_ref):
     for r in range(2):
         for c in range(GX):
             dens_ref[r, c : c + 1, :] = ob[c, r, 0:1, :]
             pres_ref[r, c : c + 1, :] = ob[c, r, 1:2, :]
             resid_ref[r, c : c + 1, :] = ob[c, r, 2:3, :]
-    wait_top()
-    peaks_ref[...] = jnp.max(p2[...], axis=0)
-
-    for wanted, copy in sends:
-        pl.when(wanted)(copy.wait_send)
-    for wait in (sent_plane, sent_tower, sent_peaks, sent_top):
-        wait()
+    peaks_ref[...] = jnp.max(p2[...], axis=0)[0, :ITERS]
 
 
 def shard(offsets, masses, counts, source):
@@ -425,11 +482,14 @@
     vmem = pl.BlockSpec(memory_space=pltpu.VMEM)
     dma = pltpu.SemaphoreType.DMA
     cells = (ROWS, SLOT, SLOT)
-    density, pressure, residual, peaks = pl.pallas_call(
+    gathered, peaks = pl.pallas_call(
         body,
-        out_shape=(block, block, block, jax.ShapeDtypeStruct((1, SLOT), F32)),
+        out_shape=(
+            jax.ShapeDtypeStruct((GX, 2, 4, SLOT), F32),
+            jax.ShapeDtypeStruct((ZLEN, 1, SLOT), F32),
+        ),
         in_specs=[vmem, vmem, pl.BlockSpec(memory_space=pltpu.SMEM), vmem],
-        out_specs=(vmem, vmem, vmem, vmem),
+        out_specs=(vmem, vmem),
         scratch_shapes=[
             pltpu.VMEM((GX, 2, 4, SLOT), F32),
             pltpu.VMEM((3, ROWS + 2, 4, SLOT), F32),
@@ -442,17 +502,15 @@
             pltpu.VMEM((ITERS, 3, 32, SLOT), F32),
             pltpu.VMEM((2, ROWS, SLOT), F32),
             pltpu.VMEM((ROWS, SLOT), F32),
-            pltpu.VMEM((24, SLOT), F32),
+            pltpu.VMEM((SLOT, SLOT), F32),
+            pltpu.VMEM((1, 2, SLOT), F32),
+            pltpu.VMEM((PLANE, 2, SLOT), F32),
+            pltpu.VMEM((1, 2, SLOT), F32),
+            pltpu.VMEM((ZLEN, 2, SLOT), F32),
             pltpu.VMEM((1, 1, SLOT), F32),
             pltpu.VMEM((PLANE, 1, SLOT), F32),
             pltpu.VMEM((1, 1, SLOT), F32),
-            pltpu.VMEM((ZLEN, 1, SLOT), F32),
-            pltpu.VMEM((1, 1, SLOT), F32),
-            pltpu.VMEM((PLANE, 1, SLOT), F32),
-            pltpu.VMEM((1, 1, SLOT), F32),
-            pltpu.VMEM((ZLEN, 1, SLOT), F32),
             pltpu.VMEM((ROWS, 4, SLOT), F32),
-            pltpu.VMEM((GX, 2, 4, SLOT), F32),
             dma((24,)),
             dma((3,)),
             dma((2,)),
@@ -466,7 +524,12 @@
         ],
         compiler_params=pltpu.CompilerParams(collective_id=0, has_side_effects=True),
     )(offsets, masses, counts, source)
-    return density, pressure, residual, peaks[0, :ITERS]
+    return pl.pallas_call(
+        finish,
+        out_shape=(block, block, block, jax.ShapeDtypeStruct((ITERS,), F32)),
+        in_specs=[vmem, vmem],
+        out_specs=(vmem, vmem, vmem, vmem),
+    )(gathered, peaks)
 
 
 def solution(mesh):

time: 69.2 us -> 68.5 us (0.990)
  local copies, waits for them, and re-layouts: 3.2 us -> 0 us
  Pallas kernels: 65 us -> 67.7 us
    pallas_call x1 -> x2, Pallas kernels: 65 us -> 67.7 us  [the longest x1 66.3 us: shard(): pl.pallas_call(body, out_shape=(jax.ShapeDtypeStruct((GX, 2, 4, SLOT), F3...]
    unnamed x9 -> x0, local copies, waits for them, and re-layouts: 2 us -> none
    squeeze x1 -> x0, local copies, waits for them, and re-layouts: 1.2 us -> none  [shard(): return (density, pressure, residual, peaks[0, :ITERS])]
where the time goes in v2:
time: 68.5 us; the launch traced here: 68.3 us
  Pallas kernels  67.7 us (99%)
    pallas_call x1, Pallas kernels, shard(): pl.pallas_call(body, out_shape=(jax.ShapeDtypeStruct((GX, 2, 4, SLOT), F3...  66.3 us
    pallas_call x1, Pallas kernels, shard(): pl.pallas_call(finish, out_shape=(block, block, block, jax.ShapeDtypeStru...  1.39 us

profile of v2, /device:TPU:1, one launch (start us, length us, event | category | flops | bytes accessed | tf_op | source)
XLA Modules:
  0.0 68.3 jit_solution(3790685195952944277)
XLA Ops:
  0.6 66.3 %shard_map.75 = (f32[8,2,4,128]{3,2,1,0:T(4,128)}, f32[8,1,128]{2,1,0:T(1,128)}) custom-call(f32[2,2,8,128]{3,2,1,0:T(8,128)} %off_ref.1, f32[2,8,128]{2,1,0:T(8,128)} %mass_ref.1, s32[2,8]{1,0:T(2,128)} %cnt_ref.1, f32[2,8,128]{2,1,0:T(8,128)} %src_ref.1), custom_call_target="tpu_custom_call" | custom-call | tf_op jit(solution)/shard_map/pallas_call | solution.py:485
  66.9 1.4 %shard_map.76 = (f32[2,8,128]{2,1,0:T(8,128)}, f32[2,8,128]{2,1,0:T(8,128)}, f32[2,8,128]{2,1,0:T(8,128)}, f32[5]{0:T(128)}) custom-call(f32[8,2,4,128]{3,2,1,0:T(4,128)} %get-tuple-element.6.ob, f32[8,1,128]{2,1,0:T(1,128)} %get-tuple-element.7.p2), custom_call_target="tpu_custom_call" | custom-call | tf_op jit(solution)/shard_map/pallas_call | solution.py:527

commit v3 on v2

--- a/solution.py
+++ b/solution.py
@@ -22,7 +22,17 @@
 FAR = 1000.0
 SHIFTS = (0.8125, 0.0625, 0.8125, 0.125, 0.5)
 PAIRS = [(i, j) for i in range(ITERS) for j in range(i, ITERS)] + [(i, ITERS) for i in range(ITERS)]
-LOOP = 4
+
+
+def hops(step, length):
+    return min(step, length - step)
+
+
+PLANE_STEPS = sorted(
+    ((dy, dx, dc) for dy in range(GX // 2) for dx in range(XLEN) for dc in range(2) if (dy, dx, dc) != (0, 0, 0)),
+    key=lambda s: -(hops(s[0], GX // 2) + hops(s[1], XLEN) + 0.5 * s[2]),
+)
+TOWER_STEPS = sorted(range(1, ZLEN), key=lambda s: -hops(s, ZLEN))
 
 
 def snake(q):
@@ -102,11 +112,12 @@
 
 
 def body(
+    off_hbm, mass_hbm, cnt_hbm, src_hbm,
+    ob, p2,
     off_ref, mass_ref, cnt_ref, src_ref,
-    ob, p2,
     sbuf, inb, xcol, ycol, rcol, wts, part, rb, vb, rows_s, ub, gb,
     g1s, g1, g2s, g2, p1s, p1, p2s, osb,
-    in_send, in_recv, rho_send, rho_recv, halo_send, halo_recv,
+    load_sem, in_send, in_recv, rho_send, rho_recv, halo_send, halo_recv,
     red_send, red_recv, out_send, out_recv,
 ):
     a, q = lax.axis_index("gx"), lax.axis_index("gy")
@@ -118,30 +129,54 @@
     left = device_of(jnp.maximum(column - 1, 0))
     right = device_of(jnp.minimum(column + 1, COLS - 1))
     plane_index = a * XLEN + x
-
-    inb[...] = jnp.zeros_like(inb)
-    rb[...] = jnp.zeros_like(rb)
-    vb[...] = jnp.zeros_like(vb)
-    osb[...] = jnp.zeros_like(osb)
-    gb[...] = jnp.zeros_like(gb)
-    part[0] = jnp.zeros((SLOT, SLOT), F32)
+    near_slot, far_slot = 2 - 2 * lax.rem(column, 2), 2 * lax.rem(column, 2)
+    has_far = (column + lax.rem(column, 2) > 0) & (column + lax.rem(column, 2) < COLS)
+
+    loads = [
+        pltpu.make_async_copy(src, dst, load_sem.at[k])
+        for k, (src, dst) in enumerate(
+            ((off_hbm, off_ref), (mass_hbm, mass_ref), (src_hbm, src_ref), (cnt_hbm, cnt_ref))
+        )
+    ]
+    for load in loads:
+        load.start()
+
+    rim = jnp.zeros((4, SLOT), F32)
+    for slot in range(3):
+        inb[slot, 0] = rim
+        inb[slot, ROWS + 1] = rim
+    wide = jnp.zeros((8, SLOT), F32)
+    for slot in range(3):
+        for end in (0, 24):
+            rb[slot, end : end + 8, :] = wide
+            for k in range(ITERS):
+                vb[k, slot, end : end + 8, :] = wide
+    for have, slot in ((has_left, 0), (has_right, 2)):
+        @pl.when(jnp.logical_not(have))
+        def _(slot=slot):
+            inb[slot] = jnp.zeros((ROWS + 2, 4, SLOT), F32)
+            rb[slot] = jnp.zeros((32, SLOT), F32)
+            for k in range(ITERS):
+                vb[k, slot] = jnp.zeros((32, SLOT), F32)
 
     barrier = pltpu.get_barrier_semaphore()
 
-    def plane_mate(t):
-        other = lax.rem(plane_index + t, PLANE)
-        return lax.div(other, XLEN), z * XLEN + lax.rem(other, XLEN)
-
-    def tower_mate(t):
-        return a, lax.rem(z + t, ZLEN) * XLEN + x
+    y, core = lax.div(a, 2), lax.rem(a, 2)
+
+    def plane_mate(step):
+        dy, dx, dc = step
+        return lax.rem(y + dy, GX // 2) * 2 + lax.rem(core + dc, 2), z * XLEN + lax.rem(x + dx, XLEN)
+
+    def tower_mate(step):
+        return a, lax.rem(z + step, ZLEN) * XLEN + x
 
     def greet(target):
         pl.semaphore_signal(barrier, inc=1, device_id=target, device_id_type=MESH)
 
-    for t in range(1, PLANE):
-        greet(plane_mate(t))
-    for t in range(1, ZLEN):
-        greet(tower_mate(t))
+    for step in TOWER_STEPS:
+        greet(tower_mate(step))
+    for step in PLANE_STEPS:
+        greet(plane_mate(step))
     low_edge = (lax.rem(column, PLANE) == 0) & has_left
     high_edge = (lax.rem(column, PLANE) == PLANE - 1) & has_right
     for edge, step in ((low_edge, -1), (high_edge, 1)):
@@ -149,6 +184,12 @@
         def _(step=step):
             for k in range(GX):
                 greet((k, group + step))
+
+    osb[...] = jnp.zeros_like(osb)
+    gb[...] = jnp.zeros_like(gb)
+    part[0] = jnp.zeros((SLOT, SLOT), F32)
+    for load in loads:
+        load.wait()
 
     lane = lax.broadcasted_iota(jnp.int32, (1, SLOT), 1)
     for r in range(2):
@@ -165,8 +206,9 @@
     pl.semaphore_wait(barrier, awaited)
 
     sends = []
-    for c in range(GX):
-        for d in (-1, 0, 1):
+    for t in (4, 3, 5, 2, 6, 1, 7, 0):
+        c = lax.rem(a + t, GX)
+        for d in (0, -1, 1):
             target_column = q * GX + c + d
             wanted = jnp.logical_and(target_column >= 0, target_column < COLS)
             ta, tq = device_of(jnp.clip(target_column, 0, COLS - 1))
@@ -211,29 +253,40 @@
         return carry
 
     def columns(r):
-        xcol[r] = spread(inb[1, r + 1, 0:1, :])
-        ycol[r] = spread(inb[1, r + 1, 1:2, :])
-        rows_s[0, pl.ds(r, 1), :] = inb[1, r + 1, 2:3, :]
-        rows_s[1, pl.ds(r, 1), :] = inb[1, r + 1, 3:4, :]
-
-    columns(0)
+        cell = inb[1, r + 1]
+        fields = spread(cell[0:1]), spread(cell[1:2]), cell
+
+        def store():
+            xcol[r], ycol[r] = fields[0], fields[1]
+            rows_s[0, pl.ds(r, 1), :] = cell[2:3]
+            rows_s[1, pl.ds(r, 1), :] = cell[3:4]
+
+        return store
+
+    columns(0)()
     pl.when(has_left)(lambda: arrived(0))
     pl.when(has_right)(lambda: arrived(2))
 
-    near = [(dc, dr) for dc in (1, 0, 2) for dr in (0, 1, 2)]
+    blocks = [(slot, dr) for slot in (1, near_slot, far_slot) for dr in (0, 1, 2)]
+    side = [0.0] * 3 + [(near_slot - 1).astype(F32)] * 3 + [(far_slot - 1).astype(F32)] * 3
 
     def density_row(r):
-        rb[1, pl.ds(8 + r, 1), :] = 1.0 + total_row(part[r])
+        row = 1.0 + total_row(part[r])
+
+        def store():
+            rb[1, pl.ds(8 + r, 1), :] = row
+
+        return store
 
     def falloffs(r, carry):
-        columns(jnp.minimum(r + 1, ROWS - 1))
-        density_row(jnp.maximum(r - 1, 0))
+        store_columns = columns(jnp.minimum(r + 1, ROWS - 1))
+        store_row = density_row(jnp.maximum(r - 1, 0))
         rows = []
-        for dc, dr in near:
-            cell = inb[dc, r + dr]
+        for (slot, dr), step_y in zip(blocks, side):
+            cell = inb[slot, r + dr]
             mass = cell[2:3, :]
             px = (dr - 1.0) + jnp.where(mass > 0.0, cell[0:1, :], FAR)
-            py = (dc - 1.0) + cell[1:2, :]
+            py = step_y + cell[1:2, :]
             rows.append((px, py, mass))
         for h in range(0, SLOT, 64):
             xi, yi = xcol[r, h : h + 64, :], ycol[r, h : h + 64, :]
@@ -245,10 +298,12 @@
                 wts[r, k, h : h + 64, :] = square
                 acc = acc + square * fall * mass
             part[r, h : h + 64, :] = acc
+        store_columns()
+        store_row()
         return carry
 
     lax.fori_loop(0, ROWS, falloffs, 0)
-    density_row(ROWS - 1)
+    density_row(ROWS - 1)()
 
     def exchange(buf, send, recv):
         copies = []
@@ -264,14 +319,19 @@
             pl.when(have)(copy.start)
             copies.append((have, copy))
 
-        def wait():
-            for have, slot in ((has_left, 0), (has_right, 2)):
-                view = buf.at[slot, pl.ds(8, ROWS)]
-                pl.when(have)(pltpu.make_async_copy(view, view, recv.at[slot]).wait)
-
-        return wait, copies
-
-    wait_rho, rho_copies = exchange(rb, rho_send, rho_recv)
+        def wait(slot):
+            view = buf.at[slot, pl.ds(8, ROWS)]
+            pltpu.make_async_copy(view, view, recv.at[slot]).wait()
+
+        def wait_near():
+            wait(near_slot)
+
+        def wait_far():
+            pl.when(has_far)(lambda: wait(far_slot))
+
+        return wait_near, wait_far, copies
+
+    wait_rho_near, wait_rho_far, rho_copies = exchange(rb, rho_send, rho_recv)
     sends += rho_copies
 
     def rho_columns(r, carry):
@@ -280,14 +340,9 @@
 
     lax.fori_loop(0, ROWS, rho_columns, 0, unroll=ROWS)
 
-    def diagonal_row(r):
-        ub[pl.ds(r, 1), :] = BASE_STIFF + total_row(part[r])
-
     def weights(first, last):
         def run(r, carry):
-            if first:
-                diagonal_row(jnp.maximum(r - 1, 0))
-            rows = [10.0 * rb[dc, pl.ds(7 + r + dr, 1), :] for dc, dr in near[first:last]]
+            rows = [10.0 * rb[slot, pl.ds(7 + r + dr, 1), :] for slot, dr in blocks[first:last]]
             for h in range(0, SLOT, 64):
                 ri = rcol[r, h : h + 64, :]
                 acc = jnp.zeros((64, SLOT), F32) if first == 0 else part[r, h : h + 64, :]
@@ -301,10 +356,17 @@
         lax.fori_loop(0, ROWS, run, 0)
 
     weights(0, 3)
-    wait_rho()
-    weights(3, 9)
-
-    diagonal_row(ROWS - 1)
+    wait_rho_near()
+    weights(3, 6)
+    wait_rho_far()
+    weights(6, 9)
+
+    def diagonal_rows(r, carry):
+        ub[pl.ds(r, 1), :] = BASE_STIFF + total_row(part[r])
+        return carry
+
+    lax.fori_loop(0, ROWS, diagonal_rows, 0, unroll=ROWS)
+
     occ = jnp.where(rows_s[0] > 0.0, 1.0, 0.0).astype(F32)
     diag = ub[...]
     dinv = occ / diag
@@ -313,7 +375,7 @@
 
     for k in range(ITERS):
         vb[k, 1, pl.ds(8, ROWS), :] = basis[k]
-        wait_halo, halo_copies = exchange(vb.at[k], halo_send.at[k], halo_recv.at[k])
+        wait_near, wait_far, halo_copies = exchange(vb.at[k], halo_send.at[k], halo_recv.at[k])
         sends += halo_copies
 
         def apply_own(r, carry):
@@ -327,17 +389,28 @@
         scaled = basis[k] * diag
         for i in range(k + 1):
             gram_rows[i, k] = jnp.sum(basis[i] * scaled, axis=0, keepdims=True)
-        wait_halo()
-
-        def apply_rest(r, carry):
+        wait_near()
+
+        def apply_near(r, carry):
             acc = part[r]
-            for m in range(3, 9):
-                dc, dr = near[m]
-                acc = acc + wts[r, m] * vb[k, dc, pl.ds(7 + r + dr, 1), :]
+            for m in range(3, 6):
+                slot, dr = blocks[m]
+                acc = acc + wts[r, m] * vb[k, slot, pl.ds(7 + r + dr, 1), :]
+            part[r] = acc
+            return carry
+
+        lax.fori_loop(0, ROWS, apply_near, 0, unroll=2)
+        wait_far()
+
+        def apply_far(r, carry):
+            acc = part[r]
+            for m in range(6, 9):
+                slot, dr = blocks[m]
+                acc = acc + wts[r, m] * vb[k, slot, pl.ds(7 + r + dr, 1), :]
             ub[pl.ds(r, 1), :] = total_row(acc)
             return carry
 
-        lax.fori_loop(0, ROWS, apply_rest, 0, unroll=ROWS)
+        lax.fori_loop(0, ROWS, apply_far, 0, unroll=ROWS)
         basis.append(2.0 * (ub[...] * dinv - SHIFTS[k] * basis[k]))
 
     scaled = basis[ITERS] * diag
@@ -356,24 +429,29 @@
     for size in (32, 16, 8, 4, 2, 1):
         gram_sum = pair_add((gram_sum[0][:size], gram_sum[1][:size]), (gram_sum[0][size:], gram_sum[1][size:]))
 
-    def gather(rows, own, all_refs, mates, index, count, send_sem, recv_sem):
+    def gather(rows, own, all_refs, mate, steps, index, send_sem, recv_sem, by_copy=False):
+        count = len(steps) + 1
+
         for k, row in enumerate(rows):
             own[0, k : k + 1, :] = row
-        for t in range(1, count):
+        for step in steps:
             copy = pltpu.make_async_remote_copy(
                 src_ref=own.at[0],
                 dst_ref=all_refs.at[index],
                 send_sem=send_sem,
                 recv_sem=recv_sem,
-                device_id=mates(t),
+                device_id=mate(step),
                 device_id_type=MESH,
             )
             copy.start()
-        for k, row in enumerate(rows):
-            all_refs[index, k : k + 1, :] = row
+        if by_copy:
+            pltpu.make_async_copy(own.at[0], all_refs.at[index], recv_sem).start()
+        else:
+            for k, row in enumerate(rows):
+                all_refs[index, k : k + 1, :] = row
 
         def wait():
-            view = all_refs.at[pl.ds(0, count - 1)]
+            view = all_refs.at[pl.ds(0, count if by_copy else count - 1)]
             pltpu.make_async_copy(view, view, recv_sem).wait()
 
         def wait_sent():
@@ -385,10 +463,10 @@
     def pairs_of(refs, count):
         return pair_tree([(refs[k, 0:1, :], refs[k, 1:2, :]) for k in range(count)])
 
-    wait_plane, sent_plane = gather(gram_sum, g1s, g1, plane_mate, plane_index, PLANE, red_send.at[0], red_recv.at[0])
+    wait_plane, sent_plane = gather(gram_sum, g1s, g1, plane_mate, PLANE_STEPS, plane_index, red_send.at[0], red_recv.at[0])
     wait_plane()
     plane_sum = pairs_of(g1, PLANE)
-    wait_tower, sent_tower = gather(plane_sum, g2s, g2, tower_mate, z, ZLEN, red_send.at[1], red_recv.at[1])
+    wait_tower, sent_tower = gather(plane_sum, g2s, g2, tower_mate, TOWER_STEPS, z, red_send.at[1], red_recv.at[1])
     wait_tower()
     total = pairs_of(g2, ZLEN)
     high, low = spread(total[0]), spread(total[1])
@@ -435,7 +513,7 @@
         gb[k : k + 1, :] = jnp.max(jnp.abs(field), axis=0, keepdims=True)
     peak = jnp.max(gb[0:8, :], axis=1, keepdims=True)
     peak_row = jnp.sum(jnp.where(sub8 == lane8, peak, 0.0), axis=0, keepdims=True)
-    wait_peaks, sent_peaks = gather([peak_row], p1s, p1, plane_mate, plane_index, PLANE, red_send.at[2], red_recv.at[2])
+    wait_peaks, sent_peaks = gather([peak_row], p1s, p1, plane_mate, PLANE_STEPS, plane_index, red_send.at[2], red_recv.at[2])
 
     density = rb[1, pl.ds(8, ROWS), :]
     for r in range(ROWS):
@@ -458,7 +536,7 @@
     pl.when(group == q)(local.start)
 
     wait_peaks()
-    wait_top, sent_top = gather([jnp.max(p1[...], axis=0)], p2s, p2, tower_mate, z, ZLEN, red_send.at[3], red_recv.at[3])
+    wait_top, sent_top = gather([jnp.max(p1[...], axis=0)], p2s, p2, tower_mate, TOWER_STEPS, z, red_send.at[3], red_recv.at[3], by_copy=True)
     pltpu.make_async_copy(ob, ob, out_recv).wait()
     wait_top()
 
@@ -485,12 +563,16 @@
     gathered, peaks = pl.pallas_call(
         body,
         out_shape=(
-            jax.ShapeDtypeStruct((GX, 2, 4, SLOT), F32),
-            jax.ShapeDtypeStruct((ZLEN, 1, SLOT), F32),
+            pltpu.VMEM((GX, 2, 4, SLOT), F32),
+            pltpu.VMEM((ZLEN, 1, SLOT), F32),
         ),
-        in_specs=[vmem, vmem, pl.BlockSpec(memory_space=pltpu.SMEM), vmem],
-        out_specs=(vmem, vmem),
+        in_specs=[pl.BlockSpec(memory_space=pl.ANY)] * 4,
+        out_specs=(pl.BlockSpec(memory_space=pl.ANY),) * 2,
         scratch_shapes=[
+            pltpu.VMEM((2, 2, GX, SLOT), F32),
+            pltpu.VMEM((2, GX, SLOT), F32),
+            pltpu.SMEM((2, GX), jnp.int32),
+            pltpu.VMEM((2, GX, SLOT), F32),
             pltpu.VMEM((GX, 2, 4, SLOT), F32),
             pltpu.VMEM((3, ROWS + 2, 4, SLOT), F32),
             pltpu.VMEM(cells, F32),
@@ -511,6 +593,7 @@
             pltpu.VMEM((PLANE, 1, SLOT), F32),
             pltpu.VMEM((1, 1, SLOT), F32),
             pltpu.VMEM((ROWS, 4, SLOT), F32),
+            dma((4,)),
             dma((24,)),
             dma((3,)),
             dma((2,)),
@@ -529,7 +612,7 @@
         out_shape=(block, block, block, jax.ShapeDtypeStruct((ITERS,), F32)),
         in_specs=[vmem, vmem],
         out_specs=(vmem, vmem, vmem, vmem),
-    )(gathered, peaks)
+    )(*(pltpu.with_memory_space_constraint(u, pltpu.VMEM) for u in (gathered, peaks)))
 
 
 def solution(mesh):

time: 68.5 us -> 61.9 us (0.904)
  Pallas kernels: 67.7 us -> 61.1 us
    pallas_call x1, Pallas kernels: 66.3 us -> 60.4 us  [shard(): pl.pallas_call(body, out_shape=(pltpu.VMEM((GX, 2, 4, SLOT), F32), pltpu....]
    pallas_call x1, Pallas kernels: 1.39 us -> 0.63 us  [shard(): pl.pallas_call(finish, out_shape=(block, block, block, jax.ShapeDtypeStru...]
where the time goes in v3:
time: 61.9 us; the launch traced here: 61.7 us
  Pallas kernels  61.1 us (99%)
  between operations  0.64 us (1%)
    pallas_call x1, Pallas kernels, shard(): pl.pallas_call(body, out_shape=(pltpu.VMEM((GX, 2, 4, SLOT), F32), pltpu....  60.4 us

profile of v3, /device:TPU:1, one launch (start us, length us, event | category | flops | bytes accessed | tf_op | source)
XLA Modules:
  0.0 61.7 jit_solution(14887556425299910506)
XLA Ops:
  0.6 60.4 %shard_map.75 = (f32[8,2,4,128]{3,2,1,0:T(4,128)S(1)}, f32[8,1,128]{2,1,0:T(1,128)S(1)}) custom-call(f32[2,2,8,128]{3,2,1,0:T(8,128)} %off_hbm.1, f32[2,8,128]{2,1,0:T(8,128)} %mass_hbm.1, s32[2,8]{1,0:T(2,128)} %cnt_hbm.1, f32[2,8,128]{2,1,0:T(8,128)} %src_hbm.1), custom_call_target="tpu_custom_call" | custom-call | tf_op jit(solution)/shard_map/pallas_call | solution.py:563
  61.1 0.6 %shard_map.76 = (f32[2,8,128]{2,1,0:T(8,128)}, f32[2,8,128]{2,1,0:T(8,128)}, f32[2,8,128]{2,1,0:T(8,128)}, f32[5]{0:T(128)}) custom-call(f32[8,2,4,128]{3,2,1,0:T(4,128)S(1)} %get-tuple-element.6.ob, f32[8,1,128]{2,1,0:T(1,128)S(1)} %get-tuple-element.7.p2), custom_call_target="tpu_custom_call" | custom-call | tf_op jit(solution)/shard_map/pallas_call | solution.py:610

commit v4 on v3

--- a/solution.py
+++ b/solution.py
@@ -41,7 +41,9 @@
 
 
 def mirrored(g, a):
-    return a + lax.rem(g, 2) * (GX - 1 - 2 * a)
+    y, core = lax.div(a, 2), lax.rem(a, 2)
+    second = lax.div(g, COLS // GX // 2)
+    return 2 * (y + lax.rem(g, 2) * (GX // 2 - 1 - 2 * y)) + core + second * (1 - 2 * core)
 
 
 def two_sum(a, b):
@@ -182,6 +184,7 @@
     for edge, step in ((low_edge, -1), (high_edge, 1)):
         @pl.when(edge)
         def _(step=step):
+            greet(left if step < 0 else right)
             for k in range(GX):
                 greet((k, group + step))
 
@@ -202,7 +205,9 @@
 
     low_block = (x == 0) & (q > 0)
     high_block = (x == XLEN - 1) & (q < COLS // GX - 1)
-    awaited = PLANE - 1 + ZLEN - 1 + low_block.astype(jnp.int32) + high_block.astype(jnp.int32)
+    awaited = PLANE - 1 + ZLEN - 1
+    for more in (low_block, high_block, low_edge, high_edge):
+        awaited = awaited + more.astype(jnp.int32)
     pl.semaphore_wait(barrier, awaited)
 
     sends = []

time: 61.9 us -> 56.6 us (0.914)
  Pallas kernels: 61.1 us -> 55.8 us
    pallas_call x1, Pallas kernels: 60.4 us -> 55.1 us  [shard(): pl.pallas_call(body, out_shape=(pltpu.VMEM((GX, 2, 4, SLOT), F32), pltpu....]
where the time goes in v4:
time: 56.6 us; the launch traced here: 56.4 us
  Pallas kernels  55.8 us (99%)
  between operations  0.64 us (1%)
    pallas_call x1, Pallas kernels, shard(): pl.pallas_call(body, out_shape=(pltpu.VMEM((GX, 2, 4, SLOT), F32), pltpu....  55.1 us

profile of v4, /device:TPU:1, one launch (start us, length us, event | category | flops | bytes accessed | tf_op | source)
XLA Modules:
  0.0 56.4 jit_solution(15685868795237787720)
XLA Ops:
  0.6 55.1 %shard_map.75 = (f32[8,2,4,128]{3,2,1,0:T(4,128)S(1)}, f32[8,1,128]{2,1,0:T(1,128)S(1)}) custom-call(f32[2,2,8,128]{3,2,1,0:T(8,128)} %off_hbm.1, f32[2,8,128]{2,1,0:T(8,128)} %mass_hbm.1, s32[2,8]{1,0:T(2,128)} %cnt_hbm.1, f32[2,8,128]{2,1,0:T(8,128)} %src_hbm.1), custom_call_target="tpu_custom_call" | custom-call | tf_op jit(solution)/shard_map/pallas_call | solution.py:568
  55.8 0.6 %shard_map.76 = (f32[2,8,128]{2,1,0:T(8,128)}, f32[2,8,128]{2,1,0:T(8,128)}, f32[2,8,128]{2,1,0:T(8,128)}, f32[5]{0:T(128)}) custom-call(f32[8,2,4,128]{3,2,1,0:T(4,128)S(1)} %get-tuple-element.6.ob, f32[8,1,128]{2,1,0:T(1,128)S(1)} %get-tuple-element.7.p2), custom_call_target="tpu_custom_call" | custom-call | tf_op jit(solution)/shard_map/pallas_call | solution.py:615

commit v5 on v4

--- a/solution.py
+++ b/solution.py
@@ -21,7 +21,7 @@
 BASE_STIFF = 0.5
 FAR = 1000.0
 SHIFTS = (0.8125, 0.0625, 0.8125, 0.125, 0.5)
-PAIRS = [(i, j) for i in range(ITERS) for j in range(i, ITERS)] + [(i, ITERS) for i in range(ITERS)]
+PAIRS = [(i, j) for i in range(ITERS) for j in range(i, ITERS)]
 
 
 def hops(step, length):
@@ -118,8 +118,8 @@
     ob, p2,
     off_ref, mass_ref, cnt_ref, src_ref,
     sbuf, inb, xcol, ycol, rcol, wts, part, rb, vb, rows_s, ub, gb,
-    g1s, g1, g2s, g2, p1s, p1, p2s, osb,
-    load_sem, in_send, in_recv, rho_send, rho_recv, halo_send, halo_recv,
+    g1s, g1, g2s, g2, b1s, b1, b2s, b2, p1s, p1, p2s, osb,
+    load_sem, in_send, in_recv, cell_send, cell_recv, rho_send, rho_recv, halo_send, halo_recv,
     red_send, red_recv, out_send, out_recv,
 ):
     a, q = lax.axis_index("gx"), lax.axis_index("gy")
@@ -175,18 +175,16 @@
     def greet(target):
         pl.semaphore_signal(barrier, inc=1, device_id=target, device_id_type=MESH)
 
+    for step in PLANE_STEPS:
+        greet(plane_mate(step))
     for step in TOWER_STEPS:
         greet(tower_mate(step))
-    for step in PLANE_STEPS:
-        greet(plane_mate(step))
     low_edge = (lax.rem(column, PLANE) == 0) & has_left
     high_edge = (lax.rem(column, PLANE) == PLANE - 1) & has_right
     for edge, step in ((low_edge, -1), (high_edge, 1)):
         @pl.when(edge)
         def _(step=step):
             greet(left if step < 0 else right)
-            for k in range(GX):
-                greet((k, group + step))
 
     osb[...] = jnp.zeros_like(osb)
     gb[...] = jnp.zeros_like(gb)
@@ -203,119 +201,33 @@
             sbuf[c, r, 2:3, :] = mass_ref[r, c : c + 1, :] * occ
             sbuf[c, r, 3:4, :] = src_ref[r, c : c + 1, :] * occ
 
-    low_block = (x == 0) & (q > 0)
-    high_block = (x == XLEN - 1) & (q < COLS // GX - 1)
-    awaited = PLANE - 1 + ZLEN - 1
-    for more in (low_block, high_block, low_edge, high_edge):
-        awaited = awaited + more.astype(jnp.int32)
+    awaited = PLANE - 1 + ZLEN - 1 + low_edge.astype(jnp.int32) + high_edge.astype(jnp.int32)
     pl.semaphore_wait(barrier, awaited)
 
     sends = []
+    home = snake(q)
     for t in (4, 3, 5, 2, 6, 1, 7, 0):
-        c = lax.rem(a + t, GX)
-        for d in (0, -1, 1):
-            target_column = q * GX + c + d
-            wanted = jnp.logical_and(target_column >= 0, target_column < COLS)
-            ta, tq = device_of(jnp.clip(target_column, 0, COLS - 1))
-            wanted = jnp.logical_and(wanted, jnp.logical_or(ta != a, tq != q))
-            copy = pltpu.make_async_remote_copy(
-                src_ref=sbuf.at[c],
-                dst_ref=inb.at[1 - d, pl.ds(1 + 2 * a, 2)],
-                send_sem=in_send.at[len(sends)],
-                recv_sem=in_recv.at[1 - d],
-                device_id=(ta, tq),
-                device_id_type=MESH,
-            )
-            pl.when(wanted)(copy.start)
-            sends.append((wanted, copy))
-    for d in (-1, 0, 1):
-        own = column + d - q * GX
-        inside = (own >= 0) & (own < GX)
-        copy = pltpu.make_async_copy(
-            sbuf.at[jnp.clip(own, 0, GX - 1)],
-            inb.at[1 + d, pl.ds(1 + 2 * a, 2)],
-            in_recv.at[1 + d],
+        target = lax.rem(a + t, GX)
+        copy = pltpu.make_async_remote_copy(
+            src_ref=sbuf.at[mirrored(q, target)],
+            dst_ref=inb.at[1, pl.ds(1 + 2 * a, 2)],
+            send_sem=in_send.at[t],
+            recv_sem=in_recv,
+            device_id=(target, home),
+            device_id_type=MESH,
         )
-        pl.when(inside)(copy.start)
-
-    def arrived(slot):
-        view = inb.at[slot, pl.ds(1, ROWS)]
-        pltpu.make_async_copy(view, view, in_recv.at[slot]).wait()
-
-    def spread(row):
-        return jnp.transpose(jnp.broadcast_to(row, (SLOT, SLOT)))
-
-    def total_row(block):
-        return jnp.sum(jnp.transpose(block), axis=0, keepdims=True)
-
-    arrived(1)
-
-    def columns(r, carry):
-        xcol[r] = spread(inb[1, r + 1, 0:1, :])
-        ycol[r] = spread(inb[1, r + 1, 1:2, :])
-        rows_s[0, pl.ds(r, 1), :] = inb[1, r + 1, 2:3, :]
-        rows_s[1, pl.ds(r, 1), :] = inb[1, r + 1, 3:4, :]
-        return carry
-
-    def columns(r):
-        cell = inb[1, r + 1]
-        fields = spread(cell[0:1]), spread(cell[1:2]), cell
-
-        def store():
-            xcol[r], ycol[r] = fields[0], fields[1]
-            rows_s[0, pl.ds(r, 1), :] = cell[2:3]
-            rows_s[1, pl.ds(r, 1), :] = cell[3:4]
-
-        return store
-
-    columns(0)()
-    pl.when(has_left)(lambda: arrived(0))
-    pl.when(has_right)(lambda: arrived(2))
-
-    blocks = [(slot, dr) for slot in (1, near_slot, far_slot) for dr in (0, 1, 2)]
-    side = [0.0] * 3 + [(near_slot - 1).astype(F32)] * 3 + [(far_slot - 1).astype(F32)] * 3
-
-    def density_row(r):
-        row = 1.0 + total_row(part[r])
-
-        def store():
-            rb[1, pl.ds(8 + r, 1), :] = row
-
-        return store
-
-    def falloffs(r, carry):
-        store_columns = columns(jnp.minimum(r + 1, ROWS - 1))
-        store_row = density_row(jnp.maximum(r - 1, 0))
-        rows = []
-        for (slot, dr), step_y in zip(blocks, side):
-            cell = inb[slot, r + dr]
-            mass = cell[2:3, :]
-            px = (dr - 1.0) + jnp.where(mass > 0.0, cell[0:1, :], FAR)
-            py = step_y + cell[1:2, :]
-            rows.append((px, py, mass))
-        for h in range(0, SLOT, 64):
-            xi, yi = xcol[r, h : h + 64, :], ycol[r, h : h + 64, :]
-            acc = jnp.zeros((64, SLOT), F32)
-            for k, (px, py, mass) in enumerate(rows):
-                ox, oy = px - xi, py - yi
-                fall = jnp.maximum(1.0 - (ox * ox + oy * oy), 0.0)
-                square = fall * fall
-                wts[r, k, h : h + 64, :] = square
-                acc = acc + square * fall * mass
-            part[r, h : h + 64, :] = acc
-        store_columns()
-        store_row()
-        return carry
-
-    lax.fori_loop(0, ROWS, falloffs, 0)
-    density_row(ROWS - 1)()
-
-    def exchange(buf, send, recv):
+        wanted = jnp.logical_or(target != a, home != q)
+        pl.when(wanted)(copy.start)
+        sends.append((wanted, copy))
+    local = pltpu.make_async_copy(sbuf.at[place], inb.at[1, pl.ds(1 + 2 * a, 2)], in_recv)
+    pl.when(home == q)(local.start)
+
+    def exchange(buf, first, send, recv):
         copies = []
         for k, (have, target, slot) in enumerate(((has_left, left, 2), (has_right, right, 0))):
             copy = pltpu.make_async_remote_copy(
-                src_ref=buf.at[1, pl.ds(8, ROWS)],
-                dst_ref=buf.at[slot, pl.ds(8, ROWS)],
+                src_ref=buf.at[1, pl.ds(first, ROWS)],
+                dst_ref=buf.at[slot, pl.ds(first, ROWS)],
                 send_sem=send.at[k],
                 recv_sem=recv.at[slot],
                 device_id=target,
@@ -325,7 +237,7 @@
             copies.append((have, copy))
 
         def wait(slot):
-            view = buf.at[slot, pl.ds(8, ROWS)]
+            view = buf.at[slot, pl.ds(first, ROWS)]
             pltpu.make_async_copy(view, view, recv.at[slot]).wait()
 
         def wait_near():
@@ -336,7 +248,79 @@
 
         return wait_near, wait_far, copies
 
-    wait_rho_near, wait_rho_far, rho_copies = exchange(rb, rho_send, rho_recv)
+    def spread(row):
+        return jnp.transpose(jnp.broadcast_to(row, (SLOT, SLOT)))
+
+    def total_row(block):
+        return jnp.sum(jnp.transpose(block), axis=0, keepdims=True)
+
+    view = inb.at[1, pl.ds(1, ROWS)]
+    pltpu.make_async_copy(view, view, in_recv).wait()
+    wait_cells_near, wait_cells_far, cell_copies = exchange(inb, 1, cell_send, cell_recv)
+    sends += cell_copies
+
+    def columns(r):
+        cell = inb[1, r + 1]
+        fields = spread(cell[0:1]), spread(cell[1:2]), cell
+
+        def store():
+            xcol[r], ycol[r] = fields[0], fields[1]
+            rows_s[0, pl.ds(r, 1), :] = cell[2:3]
+            rows_s[1, pl.ds(r, 1), :] = cell[3:4]
+
+        return store
+
+    columns(0)()
+    blocks = [(slot, dr) for slot in (1, near_slot, far_slot) for dr in (0, 1, 2)]
+    side = [0.0] * 3 + [(near_slot - 1).astype(F32)] * 3 + [(far_slot - 1).astype(F32)] * 3
+
+    def density_row(r):
+        row = 1.0 + total_row(part[r])
+
+        def store():
+            rb[1, pl.ds(8 + r, 1), :] = row
+
+        return store
+
+    def falloffs(first, last):
+        def run(r, carry):
+            if first == 0:
+                store_columns = columns(jnp.minimum(r + 1, ROWS - 1))
+            if last == 9:
+                store_row = density_row(jnp.maximum(r - 1, 0))
+            rows = []
+            for (slot, dr), step_y in zip(blocks[first:last], side[first:last]):
+                cell = inb[slot, r + dr]
+                mass = cell[2:3, :]
+                px = (dr - 1.0) + jnp.where(mass > 0.0, cell[0:1, :], FAR)
+                py = step_y + cell[1:2, :]
+                rows.append((px, py, mass))
+            for h in range(0, SLOT, 64):
+                xi, yi = xcol[r, h : h + 64, :], ycol[r, h : h + 64, :]
+                acc = jnp.zeros((64, SLOT), F32) if first == 0 else part[r, h : h + 64, :]
+                for k, (px, py, mass) in enumerate(rows, first):
+                    ox, oy = px - xi, py - yi
+                    fall = jnp.maximum(1.0 - (ox * ox + oy * oy), 0.0)
+                    square = fall * fall
+                    wts[r, k, h : h + 64, :] = square
+                    acc = acc + square * fall * mass
+                part[r, h : h + 64, :] = acc
+            if first == 0:
+                store_columns()
+            if last == 9:
+                store_row()
+            return carry
+
+        lax.fori_loop(0, ROWS, run, 0, unroll=2)
+
+    falloffs(0, 3)
+    wait_cells_near()
+    falloffs(3, 6)
+    wait_cells_far()
+    falloffs(6, 9)
+    density_row(ROWS - 1)()
+
+    wait_rho_near, wait_rho_far, rho_copies = exchange(rb, 8, rho_send, rho_recv)
     sends += rho_copies
 
     def rho_columns(r, carry):
@@ -358,7 +342,7 @@
                 part[r, h : h + 64, :] = acc
             return carry
 
-        lax.fori_loop(0, ROWS, run, 0)
+        lax.fori_loop(0, ROWS, run, 0, unroll=4)
 
     weights(0, 3)
     wait_rho_near()
@@ -377,62 +361,20 @@
     dinv = occ / diag
     basis = [rows_s[1] * dinv]
     gram_rows = {}
-
-    for k in range(ITERS):
-        vb[k, 1, pl.ds(8, ROWS), :] = basis[k]
-        wait_near, wait_far, halo_copies = exchange(vb.at[k], halo_send.at[k], halo_recv.at[k])
-        sends += halo_copies
-
-        def apply_own(r, carry):
-            acc = wts[r, 0] * vb[k, 1, pl.ds(7 + r, 1), :]
-            for m in (1, 2):
-                acc = acc + wts[r, m] * vb[k, 1, pl.ds(7 + r + m, 1), :]
-            part[r] = acc
-            return carry
-
-        lax.fori_loop(0, ROWS, apply_own, 0, unroll=2)
-        scaled = basis[k] * diag
-        for i in range(k + 1):
-            gram_rows[i, k] = jnp.sum(basis[i] * scaled, axis=0, keepdims=True)
-        wait_near()
-
-        def apply_near(r, carry):
-            acc = part[r]
-            for m in range(3, 6):
-                slot, dr = blocks[m]
-                acc = acc + wts[r, m] * vb[k, slot, pl.ds(7 + r + dr, 1), :]
-            part[r] = acc
-            return carry
-
-        lax.fori_loop(0, ROWS, apply_near, 0, unroll=2)
-        wait_far()
-
-        def apply_far(r, carry):
-            acc = part[r]
-            for m in range(6, 9):
-                slot, dr = blocks[m]
-                acc = acc + wts[r, m] * vb[k, slot, pl.ds(7 + r + dr, 1), :]
-            ub[pl.ds(r, 1), :] = total_row(acc)
-            return carry
-
-        lax.fori_loop(0, ROWS, apply_far, 0, unroll=ROWS)
-        basis.append(2.0 * (ub[...] * dinv - SHIFTS[k] * basis[k]))
-
-    scaled = basis[ITERS] * diag
-    for i in range(ITERS):
-        gram_rows[i, ITERS] = jnp.sum(basis[i] * scaled, axis=0, keepdims=True)
-
     sub8 = lax.broadcasted_iota(jnp.int32, (8, SLOT), 0)
     lane8 = lax.broadcasted_iota(jnp.int32, (8, SLOT), 1)
 
-    for i, j in PAIRS:
-        gb[8 * j + i : 8 * j + i + 1, :] = gram_rows[i, j]
-        if i != j:
-            gb[8 * i + j : 8 * i + j + 1, :] = gram_rows[i, j]
-    turned = jnp.transpose(gb[...])
-    gram_sum = two_sum(turned[:64], turned[64:])
-    for size in (32, 16, 8, 4, 2, 1):
-        gram_sum = pair_add((gram_sum[0][:size], gram_sum[1][:size]), (gram_sum[0][size:], gram_sum[1][size:]))
+    def sublane_sum(block):
+        out = two_sum(block[:64], block[64:])
+        for size in (32, 16, 8, 4, 2, 1):
+            out = pair_add((out[0][:size], out[1][:size]), (out[0][size:], out[1][size:]))
+        return out
+
+    def lane_sum(row):
+        return sublane_sum(spread(row))
+
+    def pairs_of(refs, count):
+        return pair_tree([(refs[k, 0:1, :], refs[k, 1:2, :]) for k in range(count)])
 
     def gather(rows, own, all_refs, mate, steps, index, send_sem, recv_sem, by_copy=False):
         count = len(steps) + 1
@@ -465,17 +407,72 @@
 
         return wait, wait_sent
 
-    def pairs_of(refs, count):
-        return pair_tree([(refs[k, 0:1, :], refs[k, 1:2, :]) for k in range(count)])
-
-    wait_plane, sent_plane = gather(gram_sum, g1s, g1, plane_mate, PLANE_STEPS, plane_index, red_send.at[0], red_recv.at[0])
+
+    for k in range(ITERS):
+        vb[k, 1, pl.ds(8, ROWS), :] = basis[k]
+        wait_near, wait_far, halo_copies = exchange(vb.at[k], 8, halo_send.at[k], halo_recv.at[k])
+        sends += halo_copies
+
+        def apply_own(r, carry):
+            acc = wts[r, 0] * vb[k, 1, pl.ds(7 + r, 1), :]
+            for m in (1, 2):
+                acc = acc + wts[r, m] * vb[k, 1, pl.ds(7 + r + m, 1), :]
+            part[r] = acc
+            return carry
+
+        lax.fori_loop(0, ROWS, apply_own, 0, unroll=4)
+        scaled = basis[k] * diag
+        for i in range(k + 1):
+            gram_rows[i, k] = jnp.sum(basis[i] * scaled, axis=0, keepdims=True)
+        if k == ITERS - 1:
+            for i, j in PAIRS:
+                gb[8 * j + i : 8 * j + i + 1, :] = gram_rows[i, j]
+                if i != j:
+                    gb[8 * i + j : 8 * i + j + 1, :] = gram_rows[i, j]
+            gram_sum = sublane_sum(jnp.transpose(gb[...]))
+            wait_plane, sent_plane = gather(
+                gram_sum, g1s, g1, plane_mate, PLANE_STEPS, plane_index, red_send.at[0], red_recv.at[0]
+            )
+        wait_near()
+
+        def apply_near(r, carry):
+            acc = part[r]
+            for m in range(3, 6):
+                slot, dr = blocks[m]
+                acc = acc + wts[r, m] * vb[k, slot, pl.ds(7 + r + dr, 1), :]
+            part[r] = acc
+            return carry
+
+        lax.fori_loop(0, ROWS, apply_near, 0, unroll=4)
+        wait_far()
+
+        def apply_far(r, carry):
+            acc = part[r]
+            for m in range(6, 9):
+                slot, dr = blocks[m]
+                acc = acc + wts[r, m] * vb[k, slot, pl.ds(7 + r + dr, 1), :]
+            ub[pl.ds(r, 1), :] = total_row(acc)
+            return carry
+
+        lax.fori_loop(0, ROWS, apply_far, 0, unroll=ROWS)
+        basis.append(2.0 * (ub[...] * dinv - SHIFTS[k] * basis[k]))
+
+    last_sum = lane_sum(jnp.sum(basis[ITERS - 1] * ub[...], axis=0, keepdims=True))
+    wait_last_plane, sent_last_plane = gather(
+        last_sum, b1s, b1, plane_mate, PLANE_STEPS, plane_index, red_send.at[4], red_recv.at[4]
+    )
     wait_plane()
     plane_sum = pairs_of(g1, PLANE)
     wait_tower, sent_tower = gather(plane_sum, g2s, g2, tower_mate, TOWER_STEPS, z, red_send.at[1], red_recv.at[1])
+    wait_last_plane()
+    last_plane_sum = pairs_of(b1, PLANE)
+    wait_last_tower, sent_last_tower = gather(
+        last_plane_sum, b2s, b2, tower_mate, TOWER_STEPS, z, red_send.at[5], red_recv.at[5]
+    )
     wait_tower()
     total = pairs_of(g2, ZLEN)
     high, low = spread(total[0]), spread(total[1])
-    gram = [(high[8 * j : 8 * j + 8], low[8 * j : 8 * j + 8]) for j in range(ITERS + 1)]
+    gram = [(high[8 * j : 8 * j + 8], low[8 * j : 8 * j + 8]) for j in range(ITERS)]
 
     zero = jnp.zeros((8, SLOT), F32)
     first = jnp.where(sub8 == 0, 1.0, 0.0).astype(F32)
@@ -485,6 +482,13 @@
 
     def part_of(u, k):
         return tuple(jnp.broadcast_to(w[k : k + 1], (8, SLOT)) for w in u)
+
+    shifted = zero
+    for k, shift in enumerate(SHIFTS[:-1]):
+        shifted = jnp.where(sub8 == k, 2.0 * (shift - SHIFTS[-1]), shifted)
+    following = tuple(pltpu.roll(w, 7, 0) for w in gram[ITERS - 1])
+    newest = pair_add(following, pair_scale(gram[ITERS - 1], shifted))
+    gram.append(tuple(jnp.where(sub8 < ITERS - 1, w, 0.0) for w in newest))
 
     solution_at, residual_at, direction = (zero, zero), (first, zero), (first, zero)
     residual_image = gram[0]
@@ -494,15 +498,21 @@
         moved = tuple(-0.5 * pltpu.roll(w, 1, 0) for w in direction)
         image = pair_add(pair_scale(direction, keep), moved)
         gram_image = pair_tree([pair_mul(gram[j], part_of(image, j)) for j in range(k + 2)])
-        step = pair_div(rz, pair_dot(direction, gram_image))
-        solution_at = pair_add(solution_at, pair_mul(step, direction))
-        residual_at = pair_add(residual_at, pair_neg(pair_mul(step, image)))
-        residuals.append(residual_at[0])
+        curvature = pair_dot(direction, gram_image)
         if k + 1 < ITERS:
+            step = pair_div(rz, curvature)
+            solution_at = pair_add(solution_at, pair_mul(step, direction))
+            residual_at = pair_add(residual_at, pair_neg(pair_mul(step, image)))
+            residuals.append(residual_at[0])
             residual_image = pair_add(residual_image, pair_neg(pair_mul(step, gram_image)))
             new = pair_dot(residual_at, residual_image)
             direction = pair_add(residual_at, pair_mul(pair_div(new, rz), direction))
             rz = new
+    corner = pair_mul(part_of(direction, ITERS - 1), part_of(image, ITERS))
+    corner = tuple(2.0 * w for w in corner)
+    curvature = pair_add(
+        curvature, pair_mul(corner, pair_scale(part_of(gram[ITERS - 1], ITERS - 1), -SHIFTS[-1]))
+    )
 
     def combine(factors, count):
         out = None
@@ -511,11 +521,19 @@
             out = term if out is None else out + term
         return out
 
-    pressure = combine(solution_at[0], ITERS)
     gb[0:8, :] = jnp.zeros((8, SLOT), F32)
-    for k in range(ITERS):
+    for k in range(ITERS - 1):
         field = combine(residuals[k], k + 2) * diag
         gb[k : k + 1, :] = jnp.max(jnp.abs(field), axis=0, keepdims=True)
+    pressure = combine(solution_at[0], ITERS - 1)
+    along = combine(direction[0], ITERS)
+    drop = combine(image[0], ITERS + 1) * diag
+    wait_last_tower()
+    last = tuple(jnp.broadcast_to(w, (8, SLOT)) for w in pairs_of(b2, ZLEN))
+    step = pair_div(rz, pair_add(curvature, pair_mul(corner, last)))[0][0:1]
+    pressure = pressure + step * along
+    field = field - step * drop
+    gb[ITERS - 1 : ITERS, :] = jnp.max(jnp.abs(field), axis=0, keepdims=True)
     peak = jnp.max(gb[0:8, :], axis=1, keepdims=True)
     peak_row = jnp.sum(jnp.where(sub8 == lane8, peak, 0.0), axis=0, keepdims=True)
     wait_peaks, sent_peaks = gather([peak_row], p1s, p1, plane_mate, PLANE_STEPS, plane_index, red_send.at[2], red_recv.at[2])
@@ -547,7 +565,7 @@
 
     for wanted, copy in sends:
         pl.when(wanted)(copy.wait_send)
-    for wait in (sent_plane, sent_tower, sent_peaks, sent_top):
+    for wait in (sent_plane, sent_tower, sent_last_plane, sent_last_tower, sent_peaks, sent_top):
         wait()
 
 
@@ -594,19 +612,25 @@
             pltpu.VMEM((PLANE, 2, SLOT), F32),
             pltpu.VMEM((1, 2, SLOT), F32),
             pltpu.VMEM((ZLEN, 2, SLOT), F32),
+            pltpu.VMEM((1, 2, SLOT), F32),
+            pltpu.VMEM((PLANE, 2, SLOT), F32),
+            pltpu.VMEM((1, 2, SLOT), F32),
+            pltpu.VMEM((ZLEN, 2, SLOT), F32),
             pltpu.VMEM((1, 1, SLOT), F32),
             pltpu.VMEM((PLANE, 1, SLOT), F32),
             pltpu.VMEM((1, 1, SLOT), F32),
             pltpu.VMEM((ROWS, 4, SLOT), F32),
             dma((4,)),
-            dma((24,)),
+            dma((GX,)),
+            dma,
+            dma((2,)),
             dma((3,)),
             dma((2,)),
             dma((3,)),
             dma((ITERS, 2)),
             dma((ITERS, 3)),
-            dma((4,)),
-            dma((4,)),
+            dma((6,)),
+            dma((6,)),
             dma((GX,)),
             dma,
         ],

time: 56.6 us -> 55.2 us (0.975)
  Pallas kernels: 55.8 us -> 54.4 us
    pallas_call x1, Pallas kernels: 55.1 us -> 53.8 us  [shard(): pl.pallas_call(body, out_shape=(pltpu.VMEM((GX, 2, 4, SLOT), F32), pltpu....]
where the time goes in v5:
time: 55.2 us; the launch traced here: 55.1 us
  Pallas kernels  54.4 us (99%)
  between operations  0.64 us (1%)
    pallas_call x1, Pallas kernels, shard(): pl.pallas_call(body, out_shape=(pltpu.VMEM((GX, 2, 4, SLOT), F32), pltpu....  53.8 us

profile of v5, /device:TPU:1, one launch (start us, length us, event | category | flops | bytes accessed | tf_op | source)
XLA Modules:
  0.0 55.1 jit_solution(13766480467959270721)
XLA Ops:
  0.6 53.8 %shard_map.75 = (f32[8,2,4,128]{3,2,1,0:T(4,128)S(1)}, f32[8,1,128]{2,1,0:T(1,128)S(1)}) custom-call(f32[2,2,8,128]{3,2,1,0:T(8,128)} %off_hbm.1, f32[2,8,128]{2,1,0:T(8,128)} %mass_hbm.1, s32[2,8]{1,0:T(2,128)} %cnt_hbm.1, f32[2,8,128]{2,1,0:T(8,128)} %src_hbm.1), custom_call_target="tpu_custom_call" | custom-call | tf_op jit(solution)/shard_map/pallas_call | solution.py:586
  54.4 0.6 %shard_map.76 = (f32[2,8,128]{2,1,0:T(8,128)}, f32[2,8,128]{2,1,0:T(8,128)}, f32[2,8,128]{2,1,0:T(8,128)}, f32[5]{0:T(128)}) custom-call(f32[8,2,4,128]{3,2,1,0:T(4,128)S(1)} %get-tuple-element.6.ob, f32[8,1,128]{2,1,0:T(1,128)S(1)} %get-tuple-element.7.p2), custom_call_target="tpu_custom_call" | custom-call | tf_op jit(solution)/shard_map/pallas_call | solution.py:639

commit v6 on v5

--- a/solution.py
+++ b/solution.py
@@ -32,7 +32,7 @@
     ((dy, dx, dc) for dy in range(GX // 2) for dx in range(XLEN) for dc in range(2) if (dy, dx, dc) != (0, 0, 0)),
     key=lambda s: -(hops(s[0], GX // 2) + hops(s[1], XLEN) + 0.5 * s[2]),
 )
-TOWER_STEPS = sorted(range(1, ZLEN), key=lambda s: -hops(s, ZLEN))
+TOWER_STEPS = sorted(((dz, core) for dz in range(1, ZLEN) for core in range(2)), key=lambda s: -hops(s[0], ZLEN) + 0.5 * s[1])
 
 
 def snake(q):
@@ -170,7 +170,7 @@
         return lax.rem(y + dy, GX // 2) * 2 + lax.rem(core + dc, 2), z * XLEN + lax.rem(x + dx, XLEN)
 
     def tower_mate(step):
-        return a, lax.rem(z + step, ZLEN) * XLEN + x
+        return 2 * y + step[1], lax.rem(z + step[0], ZLEN) * XLEN + x
 
     def greet(target):
         pl.semaphore_signal(barrier, inc=1, device_id=target, device_id_type=MESH)
@@ -178,7 +178,8 @@
     for step in PLANE_STEPS:
         greet(plane_mate(step))
     for step in TOWER_STEPS:
-        greet(tower_mate(step))
+        if step[1]:
+            greet(tower_mate(step))
     low_edge = (lax.rem(column, PLANE) == 0) & has_left
     high_edge = (lax.rem(column, PLANE) == PLANE - 1) & has_right
     for edge, step in ((low_edge, -1), (high_edge, 1)):
@@ -201,7 +202,7 @@
             sbuf[c, r, 2:3, :] = mass_ref[r, c : c + 1, :] * occ
             sbuf[c, r, 3:4, :] = src_ref[r, c : c + 1, :] * occ
 
-    awaited = PLANE - 1 + ZLEN - 1 + low_edge.astype(jnp.int32) + high_edge.astype(jnp.int32)
+    awaited = PLANE - 1 + 2 * (ZLEN - 1) * core + low_edge.astype(jnp.int32) + high_edge.astype(jnp.int32)
     pl.semaphore_wait(barrier, awaited)
 
     sends = []
@@ -286,8 +287,6 @@
         def run(r, carry):
             if first == 0:
                 store_columns = columns(jnp.minimum(r + 1, ROWS - 1))
-            if last == 9:
-                store_row = density_row(jnp.maximum(r - 1, 0))
             rows = []
             for (slot, dr), step_y in zip(blocks[first:last], side[first:last]):
                 cell = inb[slot, r + dr]
@@ -308,17 +307,16 @@
             if first == 0:
                 store_columns()
             if last == 9:
-                store_row()
+                density_row(r)()
             return carry
 
-        lax.fori_loop(0, ROWS, run, 0, unroll=2)
+        lax.fori_loop(0, ROWS, run, 0, unroll=16 if last == 9 else 4)
 
     falloffs(0, 3)
     wait_cells_near()
     falloffs(3, 6)
     wait_cells_far()
     falloffs(6, 9)
-    density_row(ROWS - 1)()
 
     wait_rho_near, wait_rho_far, rho_copies = exchange(rb, 8, rho_send, rho_recv)
     sends += rho_copies
@@ -340,21 +338,17 @@
                     wts[r, k, h : h + 64, :] = w
                     acc = acc + w
                 part[r, h : h + 64, :] = acc
+            if last == 9:
+                ub[pl.ds(r, 1), :] = BASE_STIFF + total_row(part[r])
             return carry
 
-        lax.fori_loop(0, ROWS, run, 0, unroll=4)
+        lax.fori_loop(0, ROWS, run, 0, unroll=ROWS if last == 9 else 4)
 
     weights(0, 3)
     wait_rho_near()
     weights(3, 6)
     wait_rho_far()
     weights(6, 9)
-
-    def diagonal_rows(r, carry):
-        ub[pl.ds(r, 1), :] = BASE_STIFF + total_row(part[r])
-        return carry
-
-    lax.fori_loop(0, ROWS, diagonal_rows, 0, unroll=ROWS)
 
     occ = jnp.where(rows_s[0] > 0.0, 1.0, 0.0).astype(F32)
     diag = ub[...]
@@ -376,21 +370,30 @@
     def pairs_of(refs, count):
         return pair_tree([(refs[k, 0:1, :], refs[k, 1:2, :]) for k in range(count)])
 
-    def gather(rows, own, all_refs, mate, steps, index, send_sem, recv_sem, by_copy=False):
-        count = len(steps) + 1
-
+    def gather(rows, own, all_refs, mate, steps, index, send_sem, recv_sem, spare=None):
         for k, row in enumerate(rows):
             own[0, k : k + 1, :] = row
-        for step in steps:
-            copy = pltpu.make_async_remote_copy(
-                src_ref=own.at[0],
-                dst_ref=all_refs.at[index],
-                send_sem=send_sem,
-                recv_sem=recv_sem,
-                device_id=mate(step),
-                device_id_type=MESH,
-            )
-            copy.start()
+
+        def send():
+            for step in steps:
+                pltpu.make_async_remote_copy(
+                    src_ref=own.at[0],
+                    dst_ref=all_refs.at[index],
+                    send_sem=send_sem,
+                    recv_sem=recv_sem,
+                    device_id=mate(step),
+                    device_id_type=MESH,
+                ).start()
+
+        def wait_sent():
+            view = (all_refs if spare is None else spare).at[pl.ds(0, len(steps))]
+            pltpu.make_async_copy(view, view, send_sem).wait()
+
+        if spare is None:
+            send()
+        else:
+            pl.when(core == 1)(send)
+        by_copy = all_refs is p2
         if by_copy:
             pltpu.make_async_copy(own.at[0], all_refs.at[index], recv_sem).start()
         else:
@@ -398,14 +401,10 @@
                 all_refs[index, k : k + 1, :] = row
 
         def wait():
-            view = all_refs.at[pl.ds(0, count if by_copy else count - 1)]
+            view = all_refs.at[pl.ds(0, all_refs.shape[0] - 1 + by_copy)]
             pltpu.make_async_copy(view, view, recv_sem).wait()
 
-        def wait_sent():
-            view = all_refs.at[pl.ds(0, count - 1)]
-            pltpu.make_async_copy(view, view, send_sem).wait()
-
-        return wait, wait_sent
+        return wait, (wait_sent if spare is None else lambda: pl.when(core == 1)(wait_sent))
 
 
     for k in range(ITERS):
@@ -463,11 +462,11 @@
     )
     wait_plane()
     plane_sum = pairs_of(g1, PLANE)
-    wait_tower, sent_tower = gather(plane_sum, g2s, g2, tower_mate, TOWER_STEPS, z, red_send.at[1], red_recv.at[1])
+    wait_tower, sent_tower = gather(plane_sum, g2s, g2, tower_mate, TOWER_STEPS, z, red_send.at[1], red_recv.at[1], g1)
     wait_last_plane()
     last_plane_sum = pairs_of(b1, PLANE)
     wait_last_tower, sent_last_tower = gather(
-        last_plane_sum, b2s, b2, tower_mate, TOWER_STEPS, z, red_send.at[5], red_recv.at[5]
+        last_plane_sum, b2s, b2, tower_mate, TOWER_STEPS, z, red_send.at[5], red_recv.at[5], b1
     )
     wait_tower()
     total = pairs_of(g2, ZLEN)
@@ -559,7 +558,7 @@
     pl.when(group == q)(local.start)
 
     wait_peaks()
-    wait_top, sent_top = gather([jnp.max(p1[...], axis=0)], p2s, p2, tower_mate, TOWER_STEPS, z, red_send.at[3], red_recv.at[3], by_copy=True)
+    wait_top, sent_top = gather([jnp.max(p1[...], axis=0)], p2s, p2, tower_mate, TOWER_STEPS, z, red_send.at[3], red_recv.at[3], p1)
     pltpu.make_async_copy(ob, ob, out_recv).wait()
     wait_top()
 

time: 55.2 us -> 53.2 us (0.964)
  Pallas kernels: 54.4 us -> 52.4 us
    pallas_call x1, Pallas kernels: 53.8 us -> 51.7 us  [shard(): pl.pallas_call(body, out_shape=(pltpu.VMEM((GX, 2, 4, SLOT), F32), pltpu....]
where the time goes in v6:
time: 53.2 us; the launch traced here: 53 us
  Pallas kernels  52.4 us (98%)
  between operations  0.64 us (1%)
    pallas_call x1, Pallas kernels, shard(): pl.pallas_call(body, out_shape=(pltpu.VMEM((GX, 2, 4, SLOT), F32), pltpu....  51.7 us

profile of v6, /device:TPU:1, one launch (start us, length us, event | category | flops | bytes accessed | tf_op | source)
XLA Modules:
  0.0 53.0 jit_solution(13432515044168116811)
XLA Ops:
  0.6 51.7 %shard_map.75 = (f32[8,2,4,128]{3,2,1,0:T(4,128)S(1)}, f32[8,1,128]{2,1,0:T(1,128)S(1)}) custom-call(f32[2,2,8,128]{3,2,1,0:T(8,128)} %off_hbm.1, f32[2,8,128]{2,1,0:T(8,128)} %mass_hbm.1, s32[2,8]{1,0:T(2,128)} %cnt_hbm.1, f32[2,8,128]{2,1,0:T(8,128)} %src_hbm.1), custom_call_target="tpu_custom_call" | custom-call | tf_op jit(solution)/shard_map/pallas_call | solution.py:585
  52.4 0.6 %shard_map.76 = (f32[2,8,128]{2,1,0:T(8,128)}, f32[2,8,128]{2,1,0:T(8,128)}, f32[2,8,128]{2,1,0:T(8,128)}, f32[5]{0:T(128)}) custom-call(f32[8,2,4,128]{3,2,1,0:T(4,128)S(1)} %get-tuple-element.6.ob, f32[8,1,128]{2,1,0:T(1,128)S(1)} %get-tuple-element.7.p2), custom_call_target="tpu_custom_call" | custom-call | tf_op jit(solution)/shard_map/pallas_call | solution.py:638

commit v7 on v6

--- a/solution.py
+++ b/solution.py
@@ -1,5 +1,3 @@
-import functools
-
 import jax
 import jax.numpy as jnp
 from jax import lax
@@ -32,6 +30,10 @@
     ((dy, dx, dc) for dy in range(GX // 2) for dx in range(XLEN) for dc in range(2) if (dy, dx, dc) != (0, 0, 0)),
     key=lambda s: -(hops(s[0], GX // 2) + hops(s[1], XLEN) + 0.5 * s[2]),
 )
+WALL_STEPS = sorted(
+    ((dy, dc, dz) for dy in range(GX // 2) for dc in range(2) for dz in range(ZLEN) if (dy, dc, dz) != (0, 0, 0)),
+    key=lambda s: -(hops(s[0], GX // 2) + 0.5 * s[1] + hops(s[2], ZLEN)),
+)
 TOWER_STEPS = sorted(((dz, core) for dz in range(1, ZLEN) for core in range(2)), key=lambda s: -hops(s[0], ZLEN) + 0.5 * s[1])
 
 
@@ -115,12 +117,12 @@
 
 def body(
     off_hbm, mass_hbm, cnt_hbm, src_hbm,
-    ob, p2,
+    ob, p1,
     off_ref, mass_ref, cnt_ref, src_ref,
     sbuf, inb, xcol, ycol, rcol, wts, part, rb, vb, rows_s, ub, gb,
-    g1s, g1, g2s, g2, b1s, b1, b2s, b2, p1s, p1, p2s, osb,
+    g1s, g1, g2s, g2, b1s, b1, b2s, b2, p1s, osb, tb,
     load_sem, in_send, in_recv, cell_send, cell_recv, rho_send, rho_recv, halo_send, halo_recv,
-    red_send, red_recv, out_send, out_recv,
+    red_send, red_recv, row_send, row_recv, out_send, out_recv,
 ):
     a, q = lax.axis_index("gx"), lax.axis_index("gy")
     z, x = lax.div(q, XLEN), lax.rem(q, XLEN)
@@ -172,6 +174,10 @@
     def tower_mate(step):
         return 2 * y + step[1], lax.rem(z + step[0], ZLEN) * XLEN + x
 
+    def wall_mate(step):
+        dy, dc, dz = step
+        return lax.rem(y + dy, GX // 2) * 2 + lax.rem(core + dc, 2), lax.rem(z + dz, ZLEN) * XLEN + x
+
     def greet(target):
         pl.semaphore_signal(barrier, inc=1, device_id=target, device_id_type=MESH)
 
@@ -182,10 +188,10 @@
             greet(tower_mate(step))
     low_edge = (lax.rem(column, PLANE) == 0) & has_left
     high_edge = (lax.rem(column, PLANE) == PLANE - 1) & has_right
-    for edge, step in ((low_edge, -1), (high_edge, 1)):
+    for edge, target in ((low_edge, left), (high_edge, right)):
         @pl.when(edge)
-        def _(step=step):
-            greet(left if step < 0 else right)
+        def _(target=target):
+            greet(target)
 
     osb[...] = jnp.zeros_like(osb)
     gb[...] = jnp.zeros_like(gb)
@@ -393,7 +399,7 @@
             send()
         else:
             pl.when(core == 1)(send)
-        by_copy = all_refs is p2
+        by_copy = all_refs is p1
         if by_copy:
             pltpu.make_async_copy(own.at[0], all_refs.at[index], recv_sem).start()
         else:
@@ -406,6 +412,22 @@
 
         return wait, (wait_sent if spare is None else lambda: pl.when(core == 1)(wait_sent))
 
+
+    def replicate(k):
+        tb[k, x] = basis[k] * diag
+        for step in (2, 1, 3):
+            pltpu.make_async_remote_copy(
+                src_ref=tb.at[k, x],
+                dst_ref=tb.at[k, x],
+                send_sem=row_send.at[k],
+                recv_sem=row_recv.at[k],
+                device_id=(a, z * XLEN + lax.rem(x + step, XLEN)),
+                device_id_type=MESH,
+            ).start()
+
+    def wait_replicas(k, sem):
+        view = tb.at[k, pl.ds(0, XLEN - 1)]
+        pltpu.make_async_copy(view, view, sem.at[k]).wait()
 
     for k in range(ITERS):
         vb[k, 1, pl.ds(8, ROWS), :] = basis[k]
@@ -420,6 +442,7 @@
             return carry
 
         lax.fori_loop(0, ROWS, apply_own, 0, unroll=4)
+        replicate(k)
         scaled = basis[k] * diag
         for i in range(k + 1):
             gram_rows[i, k] = jnp.sum(basis[i] * scaled, axis=0, keepdims=True)
@@ -460,6 +483,7 @@
     wait_last_plane, sent_last_plane = gather(
         last_sum, b1s, b1, plane_mate, PLANE_STEPS, plane_index, red_send.at[4], red_recv.at[4]
     )
+    replicate(ITERS)
     wait_plane()
     plane_sum = pairs_of(g1, PLANE)
     wait_tower, sent_tower = gather(plane_sum, g2s, g2, tower_mate, TOWER_STEPS, z, red_send.at[1], red_recv.at[1], g1)
@@ -520,22 +544,46 @@
             out = term if out is None else out + term
         return out
 
-    gb[0:8, :] = jnp.zeros((8, SLOT), F32)
-    for k in range(ITERS - 1):
-        field = combine(residuals[k], k + 2) * diag
-        gb[k : k + 1, :] = jnp.max(jnp.abs(field), axis=0, keepdims=True)
+    field = combine(residuals[-1], ITERS) * diag
+    drop = combine(image[0], ITERS + 1) * diag
     pressure = combine(solution_at[0], ITERS - 1)
     along = combine(direction[0], ITERS)
-    drop = combine(image[0], ITERS + 1) * diag
+    for k in range(ITERS + 1):
+        wait_replicas(k, row_recv)
+
+    def row_combine(factors, count, t):
+        out = None
+        for j in range(count):
+            term = factors[j : j + 1] * tb[j, t]
+            out = term if out is None else out + term
+        return out
+
+    gb[0:8, :] = jnp.zeros((8, SLOT), F32)
+    peaks = [None] * ITERS
+
+    def raise_peak(k, values):
+        values = jnp.abs(values)
+        peaks[k] = values if peaks[k] is None else jnp.maximum(peaks[k], values)
+
+    row_fields = []
+    for t in range(XLEN):
+        for k in range(ITERS - 1):
+            values = row_combine(residuals[k], k + 2, t)
+            raise_peak(k, values)
+        row_fields.append((values, row_combine(image[0], ITERS + 1, t)))
+    for k in range(ITERS - 1):
+        gb[k : k + 1, :] = jnp.max(peaks[k], axis=0, keepdims=True)
     wait_last_tower()
     last = tuple(jnp.broadcast_to(w, (8, SLOT)) for w in pairs_of(b2, ZLEN))
     step = pair_div(rz, pair_add(curvature, pair_mul(corner, last)))[0][0:1]
     pressure = pressure + step * along
     field = field - step * drop
-    gb[ITERS - 1 : ITERS, :] = jnp.max(jnp.abs(field), axis=0, keepdims=True)
+    for values, change in row_fields:
+        raise_peak(ITERS - 1, values - step * change)
+    gb[ITERS - 1 : ITERS, :] = jnp.max(peaks[ITERS - 1], axis=0, keepdims=True)
     peak = jnp.max(gb[0:8, :], axis=1, keepdims=True)
     peak_row = jnp.sum(jnp.where(sub8 == lane8, peak, 0.0), axis=0, keepdims=True)
-    wait_peaks, sent_peaks = gather([peak_row], p1s, p1, plane_mate, PLANE_STEPS, plane_index, red_send.at[2], red_recv.at[2])
+    wait_peaks, sent_peaks = gather([peak_row], p1s, p1, wall_mate, WALL_STEPS, a * ZLEN + z, red_send.at[2], red_recv.at[2])
 
     density = rb[1, pl.ds(8, ROWS), :]
     for r in range(ROWS):
@@ -558,23 +606,23 @@
     pl.when(group == q)(local.start)
 
     wait_peaks()
-    wait_top, sent_top = gather([jnp.max(p1[...], axis=0)], p2s, p2, tower_mate, TOWER_STEPS, z, red_send.at[3], red_recv.at[3], p1)
     pltpu.make_async_copy(ob, ob, out_recv).wait()
-    wait_top()
 
     for wanted, copy in sends:
         pl.when(wanted)(copy.wait_send)
-    for wait in (sent_plane, sent_tower, sent_last_plane, sent_last_tower, sent_peaks, sent_top):
+    for wait in (sent_plane, sent_tower, sent_last_plane, sent_last_tower, sent_peaks):
         wait()
-
-
-def finish(ob, p2, dens_ref, pres_ref, resid_ref, peaks_ref):
+    for k in range(ITERS + 1):
+        wait_replicas(k, row_send)
+
+
+def finish(ob, p1, dens_ref, pres_ref, resid_ref, peaks_ref):
     for r in range(2):
         for c in range(GX):
             dens_ref[r, c : c + 1, :] = ob[c, r, 0:1, :]
             pres_ref[r, c : c + 1, :] = ob[c, r, 1:2, :]
             resid_ref[r, c : c + 1, :] = ob[c, r, 2:3, :]
-    peaks_ref[...] = jnp.max(p2[...], axis=0)[0, :ITERS]
+    peaks_ref[...] = jnp.max(p1[...], axis=0)[0, :ITERS]
 
 
 def shard(offsets, masses, counts, source):
@@ -586,7 +634,7 @@
         body,
         out_shape=(
             pltpu.VMEM((GX, 2, 4, SLOT), F32),
-            pltpu.VMEM((ZLEN, 1, SLOT), F32),
+            pltpu.VMEM((GX * ZLEN, 1, SLOT), F32),
         ),
         in_specs=[pl.BlockSpec(memory_space=pl.ANY)] * 4,
         out_specs=(pl.BlockSpec(memory_space=pl.ANY),) * 2,
@@ -616,9 +664,8 @@
             pltpu.VMEM((1, 2, SLOT), F32),
             pltpu.VMEM((ZLEN, 2, SLOT), F32),
             pltpu.VMEM((1, 1, SLOT), F32),
-            pltpu.VMEM((PLANE, 1, SLOT), F32),
-            pltpu.VMEM((1, 1, SLOT), F32),
             pltpu.VMEM((ROWS, 4, SLOT), F32),
+            pltpu.VMEM((ITERS + 1, XLEN, ROWS, SLOT), F32),
             dma((4,)),
             dma((GX,)),
             dma,
@@ -630,6 +677,8 @@
             dma((ITERS, 3)),
             dma((6,)),
             dma((6,)),
+            dma((ITERS + 1,)),
+            dma((ITERS + 1,)),
             dma((GX,)),
             dma,
         ],

time: 53.2 us -> 50.9 us (0.957)
  Pallas kernels: 52.4 us -> 50.1 us
    pallas_call x1, Pallas kernels: 51.7 us -> 49.4 us  [shard(): pl.pallas_call(body, out_shape=(pltpu.VMEM((GX, 2, 4, SLOT), F32), pltpu....]
where the time goes in v7:
time: 50.9 us; the launch traced here: 50.7 us
  Pallas kernels  50.1 us (98%)
  between operations  0.64 us (1%)
    pallas_call x1, Pallas kernels, shard(): pl.pallas_call(body, out_shape=(pltpu.VMEM((GX, 2, 4, SLOT), F32), pltpu....  49.4 us

profile of v7, /device:TPU:1, one launch (start us, length us, event | category | flops | bytes accessed | tf_op | source)
XLA Modules:
  0.0 50.7 jit_solution(14459960745542020071)
XLA Ops:
  0.6 49.4 %shard_map.75 = (f32[8,2,4,128]{3,2,1,0:T(4,128)S(1)}, f32[64,1,128]{2,1,0:T(1,128)S(1)}) custom-call(f32[2,2,8,128]{3,2,1,0:T(8,128)} %off_hbm.1, f32[2,8,128]{2,1,0:T(8,128)} %mass_hbm.1, s32[2,8]{1,0:T(2,128)} %cnt_hbm.1, f32[2,8,128]{2,1,0:T(8,128)} %src_hbm.1), custom_call_target="tpu_custom_call" | custom-call | tf_op jit(solution)/shard_map/pallas_call | solution.py:633
  50.1 0.6 %shard_map.76 = (f32[2,8,128]{2,1,0:T(8,128)}, f32[2,8,128]{2,1,0:T(8,128)}, f32[2,8,128]{2,1,0:T(8,128)}, f32[5]{0:T(128)}) custom-call(f32[8,2,4,128]{3,2,1,0:T(4,128)S(1)} %get-tuple-element.6.ob, f32[64,1,128]{2,1,0:T(1,128)S(1)} %get-tuple-element.7.p1), custom_call_target="tpu_custom_call" | custom-call | tf_op jit(solution)/shard_map/pallas_call | solution.py:687

commit v8 on v7

--- a/solution.py
+++ b/solution.py
@@ -31,8 +31,8 @@
     key=lambda s: -(hops(s[0], GX // 2) + hops(s[1], XLEN) + 0.5 * s[2]),
 )
 WALL_STEPS = sorted(
-    ((dy, dc, dz) for dy in range(GX // 2) for dc in range(2) for dz in range(ZLEN) if (dy, dc, dz) != (0, 0, 0)),
-    key=lambda s: -(hops(s[0], GX // 2) + 0.5 * s[1] + hops(s[2], ZLEN)),
+    ((dy, core, dz) for dy in range(GX // 2) for core in range(2) for dz in range(ZLEN) if (dy, dz) != (0, 0)),
+    key=lambda s: -(hops(s[0], GX // 2) - 0.5 * s[1] + hops(s[2], ZLEN)),
 )
 TOWER_STEPS = sorted(((dz, core) for dz in range(1, ZLEN) for core in range(2)), key=lambda s: -hops(s[0], ZLEN) + 0.5 * s[1])
 
@@ -145,6 +145,36 @@
     for load in loads:
         load.start()
 
+    barrier = pltpu.get_barrier_semaphore()
+
+    y, core = lax.div(a, 2), lax.rem(a, 2)
+
+    def plane_mate(step):
+        dy, dx, dc = step
+        return lax.rem(y + dy, GX // 2) * 2 + lax.rem(core + dc, 2), z * XLEN + lax.rem(x + dx, XLEN)
+
+    def tower_mate(step):
+        return 2 * y + step[1], lax.rem(z + step[0], ZLEN) * XLEN + x
+
+    def wall_mate(step):
+        dy, there, dz = step
+        return lax.rem(y + dy, GX // 2) * 2 + there, lax.rem(z + dz, ZLEN) * XLEN + x
+
+    def greet(target):
+        pl.semaphore_signal(barrier, inc=1, device_id=target, device_id_type=MESH)
+
+    for step in PLANE_STEPS:
+        greet(plane_mate(step))
+    for step in TOWER_STEPS:
+        if step[1]:
+            greet(tower_mate(step))
+    low_edge = (lax.rem(column, PLANE) == 0) & has_left
+    high_edge = (lax.rem(column, PLANE) == PLANE - 1) & has_right
+    for edge, target in ((low_edge, left), (high_edge, right)):
+        @pl.when(edge)
+        def _(target=target):
+            greet(target)
+
     rim = jnp.zeros((4, SLOT), F32)
     for slot in range(3):
         inb[slot, 0] = rim
@@ -162,36 +192,6 @@
             rb[slot] = jnp.zeros((32, SLOT), F32)
             for k in range(ITERS):
                 vb[k, slot] = jnp.zeros((32, SLOT), F32)
-
-    barrier = pltpu.get_barrier_semaphore()
-
-    y, core = lax.div(a, 2), lax.rem(a, 2)
-
-    def plane_mate(step):
-        dy, dx, dc = step
-        return lax.rem(y + dy, GX // 2) * 2 + lax.rem(core + dc, 2), z * XLEN + lax.rem(x + dx, XLEN)
-
-    def tower_mate(step):
-        return 2 * y + step[1], lax.rem(z + step[0], ZLEN) * XLEN + x
-
-    def wall_mate(step):
-        dy, dc, dz = step
-        return lax.rem(y + dy, GX // 2) * 2 + lax.rem(core + dc, 2), lax.rem(z + dz, ZLEN) * XLEN + x
-
-    def greet(target):
-        pl.semaphore_signal(barrier, inc=1, device_id=target, device_id_type=MESH)
-
-    for step in PLANE_STEPS:
-        greet(plane_mate(step))
-    for step in TOWER_STEPS:
-        if step[1]:
-            greet(tower_mate(step))
-    low_edge = (lax.rem(column, PLANE) == 0) & has_left
-    high_edge = (lax.rem(column, PLANE) == PLANE - 1) & has_right
-    for edge, target in ((low_edge, left), (high_edge, right)):
-        @pl.when(edge)
-        def _(target=target):
-            greet(target)
 
     osb[...] = jnp.zeros_like(osb)
     gb[...] = jnp.zeros_like(gb)
@@ -316,7 +316,7 @@
                 density_row(r)()
             return carry
 
-        lax.fori_loop(0, ROWS, run, 0, unroll=16 if last == 9 else 4)
+        lax.fori_loop(0, ROWS, run, 0, unroll=ROWS)
 
     falloffs(0, 3)
     wait_cells_near()
@@ -392,8 +392,10 @@
                 ).start()
 
         def wait_sent():
-            view = (all_refs if spare is None else spare).at[pl.ds(0, len(steps))]
-            pltpu.make_async_copy(view, view, send_sem).wait()
+            source = all_refs if spare is None else spare
+            for start in range(0, len(steps), PLANE - 1):
+                view = source.at[pl.ds(0, min(PLANE - 1, len(steps) - start))]
+                pltpu.make_async_copy(view, view, send_sem).wait()
 
         if spare is None:
             send()
@@ -414,19 +416,20 @@
 
 
     def replicate(k):
-        tb[k, x] = basis[k] * diag
-        for step in (2, 1, 3):
+        here = 2 * x + core
+        tb[k, here] = basis[k] * diag
+        for dx, dc in ((2, 1), (2, 0), (1, 1), (3, 1), (1, 0), (3, 0), (0, 1)):
             pltpu.make_async_remote_copy(
-                src_ref=tb.at[k, x],
-                dst_ref=tb.at[k, x],
+                src_ref=tb.at[k, here],
+                dst_ref=tb.at[k, here],
                 send_sem=row_send.at[k],
                 recv_sem=row_recv.at[k],
-                device_id=(a, z * XLEN + lax.rem(x + step, XLEN)),
+                device_id=(2 * y + lax.rem(core + dc, 2), z * XLEN + lax.rem(x + dx, XLEN)),
                 device_id_type=MESH,
             ).start()
 
     def wait_replicas(k, sem):
-        view = tb.at[k, pl.ds(0, XLEN - 1)]
+        view = tb.at[k, pl.ds(0, 2 * XLEN - 1)]
         pltpu.make_async_copy(view, view, sem.at[k]).wait()
 
     for k in range(ITERS):
@@ -566,7 +569,7 @@
         peaks[k] = values if peaks[k] is None else jnp.maximum(peaks[k], values)
 
     row_fields = []
-    for t in range(XLEN):
+    for t in range(2 * XLEN):
         for k in range(ITERS - 1):
             values = row_combine(residuals[k], k + 2, t)
             raise_peak(k, values)
@@ -583,7 +586,9 @@
     gb[ITERS - 1 : ITERS, :] = jnp.max(peaks[ITERS - 1], axis=0, keepdims=True)
     peak = jnp.max(gb[0:8, :], axis=1, keepdims=True)
     peak_row = jnp.sum(jnp.where(sub8 == lane8, peak, 0.0), axis=0, keepdims=True)
-    wait_peaks, sent_peaks = gather([peak_row], p1s, p1, wall_mate, WALL_STEPS, a * ZLEN + z, red_send.at[2], red_recv.at[2])
+    wait_peaks, sent_peaks = gather(
+        [peak_row], p1s, p1, wall_mate, WALL_STEPS, y * ZLEN + z, red_send.at[2], red_recv.at[2], p1
+    )
 
     density = rb[1, pl.ds(8, ROWS), :]
     for r in range(ROWS):
@@ -634,7 +639,7 @@
         body,
         out_shape=(
             pltpu.VMEM((GX, 2, 4, SLOT), F32),
-            pltpu.VMEM((GX * ZLEN, 1, SLOT), F32),
+            pltpu.VMEM((GX // 2 * ZLEN, 1, SLOT), F32),
         ),
         in_specs=[pl.BlockSpec(memory_space=pl.ANY)] * 4,
         out_specs=(pl.BlockSpec(memory_space=pl.ANY),) * 2,
@@ -665,7 +670,7 @@
             pltpu.VMEM((ZLEN, 2, SLOT), F32),
             pltpu.VMEM((1, 1, SLOT), F32),
             pltpu.VMEM((ROWS, 4, SLOT), F32),
-            pltpu.VMEM((ITERS + 1, XLEN, ROWS, SLOT), F32),
+            pltpu.VMEM((ITERS + 1, 2 * XLEN, ROWS, SLOT), F32),
             dma((4,)),
             dma((GX,)),
             dma,

time: 50.9 us -> 50.4 us (level)
  no operation moved by 1% of the time
where the time goes in v8:
time: 50.4 us; the launch traced here: 50.2 us
  Pallas kernels  49.6 us (98%)
  between operations  0.64 us (1%)
    pallas_call x1, Pallas kernels, shard(): pl.pallas_call(body, out_shape=(pltpu.VMEM((GX, 2, 4, SLOT), F32), pltpu....  48.9 us

profile of v8, /device:TPU:1, one launch (start us, length us, event | category | flops | bytes accessed | tf_op | source)
XLA Modules:
  0.0 50.2 jit_solution(356658381638947663)
XLA Ops:
  0.6 48.9 %shard_map.75 = (f32[8,2,4,128]{3,2,1,0:T(4,128)S(1)}, f32[32,1,128]{2,1,0:T(1,128)S(1)}) custom-call(f32[2,2,8,128]{3,2,1,0:T(8,128)} %off_hbm.1, f32[2,8,128]{2,1,0:T(8,128)} %mass_hbm.1, s32[2,8]{1,0:T(2,128)} %cnt_hbm.1, f32[2,8,128]{2,1,0:T(8,128)} %src_hbm.1), custom_call_target="tpu_custom_call" | custom-call | tf_op jit(solution)/shard_map/pallas_call | solution.py:638
  49.6 0.6 %shard_map.76 = (f32[2,8,128]{2,1,0:T(8,128)}, f32[2,8,128]{2,1,0:T(8,128)}, f32[2,8,128]{2,1,0:T(8,128)}, f32[5]{0:T(128)}) custom-call(f32[8,2,4,128]{3,2,1,0:T(4,128)S(1)} %get-tuple-element.6.ob, f32[32,1,128]{2,1,0:T(1,128)S(1)} %get-tuple-element.7.p1), custom_call_target="tpu_custom_call" | custom-call | tf_op jit(solution)/shard_map/pallas_call | solution.py:692

commit v9 on v8

--- a/solution.py
+++ b/solution.py
@@ -218,34 +218,31 @@
         copy = pltpu.make_async_remote_copy(
             src_ref=sbuf.at[mirrored(q, target)],
             dst_ref=inb.at[1, pl.ds(1 + 2 * a, 2)],
-            send_sem=in_send.at[t],
+            send_sem=in_send,
             recv_sem=in_recv,
             device_id=(target, home),
             device_id_type=MESH,
         )
         wanted = jnp.logical_or(target != a, home != q)
         pl.when(wanted)(copy.start)
-        sends.append((wanted, copy))
     local = pltpu.make_async_copy(sbuf.at[place], inb.at[1, pl.ds(1 + 2 * a, 2)], in_recv)
     pl.when(home == q)(local.start)
 
     def exchange(buf, first, send, recv):
-        copies = []
-        for k, (have, target, slot) in enumerate(((has_left, left, 2), (has_right, right, 0))):
+        for have, target, slot in ((has_left, left, 2), (has_right, right, 0)):
             copy = pltpu.make_async_remote_copy(
                 src_ref=buf.at[1, pl.ds(first, ROWS)],
                 dst_ref=buf.at[slot, pl.ds(first, ROWS)],
-                send_sem=send.at[k],
-                recv_sem=recv.at[slot],
+                send_sem=send,
+                recv_sem=recv.at[slot // 2],
                 device_id=target,
                 device_id_type=MESH,
             )
             pl.when(have)(copy.start)
-            copies.append((have, copy))
 
         def wait(slot):
             view = buf.at[slot, pl.ds(first, ROWS)]
-            pltpu.make_async_copy(view, view, recv.at[slot]).wait()
+            pltpu.make_async_copy(view, view, recv.at[lax.div(slot, 2)]).wait()
 
         def wait_near():
             wait(near_slot)
@@ -253,7 +250,13 @@
         def wait_far():
             pl.when(has_far)(lambda: wait(far_slot))
 
-        return wait_near, wait_far, copies
+        def wait_sent():
+            one, both = buf.at[1, pl.ds(first, ROWS)], buf.at[pl.ds(0, 2), pl.ds(first, ROWS)]
+            inner = has_left & has_right
+            pl.when(inner)(pltpu.make_async_copy(both, both, send).wait)
+            pl.when(jnp.logical_not(inner))(pltpu.make_async_copy(one, one, send).wait)
+
+        return wait_near, wait_far, wait_sent
 
     def spread(row):
         return jnp.transpose(jnp.broadcast_to(row, (SLOT, SLOT)))
@@ -263,8 +266,8 @@
 
     view = inb.at[1, pl.ds(1, ROWS)]
     pltpu.make_async_copy(view, view, in_recv).wait()
-    wait_cells_near, wait_cells_far, cell_copies = exchange(inb, 1, cell_send, cell_recv)
-    sends += cell_copies
+    wait_cells_near, wait_cells_far, cells_sent = exchange(inb, 1, cell_send, cell_recv)
+    sends.append(cells_sent)
 
     def columns(r):
         cell = inb[1, r + 1]
@@ -324,8 +327,8 @@
     wait_cells_far()
     falloffs(6, 9)
 
-    wait_rho_near, wait_rho_far, rho_copies = exchange(rb, 8, rho_send, rho_recv)
-    sends += rho_copies
+    wait_rho_near, wait_rho_far, rho_sent = exchange(rb, 8, rho_send, rho_recv)
+    sends.append(rho_sent)
 
     def rho_columns(r, carry):
         rcol[r] = spread(10.0 * rb[1, pl.ds(8 + r, 1), :])
@@ -376,7 +379,7 @@
     def pairs_of(refs, count):
         return pair_tree([(refs[k, 0:1, :], refs[k, 1:2, :]) for k in range(count)])
 
-    def gather(rows, own, all_refs, mate, steps, index, send_sem, recv_sem, spare=None):
+    def gather(rows, own, all_refs, mate, steps, index, recv_sem, everyone):
         for k, row in enumerate(rows):
             own[0, k : k + 1, :] = row
 
@@ -385,19 +388,13 @@
                 pltpu.make_async_remote_copy(
                     src_ref=own.at[0],
                     dst_ref=all_refs.at[index],
-                    send_sem=send_sem,
+                    send_sem=red_send,
                     recv_sem=recv_sem,
                     device_id=mate(step),
                     device_id_type=MESH,
                 ).start()
 
-        def wait_sent():
-            source = all_refs if spare is None else spare
-            for start in range(0, len(steps), PLANE - 1):
-                view = source.at[pl.ds(0, min(PLANE - 1, len(steps) - start))]
-                pltpu.make_async_copy(view, view, send_sem).wait()
-
-        if spare is None:
+        if everyone:
             send()
         else:
             pl.when(core == 1)(send)
@@ -412,7 +409,7 @@
             view = all_refs.at[pl.ds(0, all_refs.shape[0] - 1 + by_copy)]
             pltpu.make_async_copy(view, view, recv_sem).wait()
 
-        return wait, (wait_sent if spare is None else lambda: pl.when(core == 1)(wait_sent))
+        return wait
 
 
     def replicate(k):
@@ -422,20 +419,20 @@
             pltpu.make_async_remote_copy(
                 src_ref=tb.at[k, here],
                 dst_ref=tb.at[k, here],
-                send_sem=row_send.at[k],
-                recv_sem=row_recv.at[k],
+                send_sem=row_send,
+                recv_sem=row_recv,
                 device_id=(2 * y + lax.rem(core + dc, 2), z * XLEN + lax.rem(x + dx, XLEN)),
                 device_id_type=MESH,
             ).start()
 
-    def wait_replicas(k, sem):
-        view = tb.at[k, pl.ds(0, 2 * XLEN - 1)]
-        pltpu.make_async_copy(view, view, sem.at[k]).wait()
+    def wait_replicas(sem):
+        view = tb.at[:, pl.ds(0, 2 * XLEN - 1)]
+        pltpu.make_async_copy(view, view, sem).wait()
 
     for k in range(ITERS):
         vb[k, 1, pl.ds(8, ROWS), :] = basis[k]
-        wait_near, wait_far, halo_copies = exchange(vb.at[k], 8, halo_send.at[k], halo_recv.at[k])
-        sends += halo_copies
+        wait_near, wait_far, halo_sent = exchange(vb.at[k], 8, halo_send.at[k], halo_recv.at[k])
+        sends.append(halo_sent)
 
         def apply_own(r, carry):
             acc = wts[r, 0] * vb[k, 1, pl.ds(7 + r, 1), :]
@@ -455,8 +452,8 @@
                 if i != j:
                     gb[8 * i + j : 8 * i + j + 1, :] = gram_rows[i, j]
             gram_sum = sublane_sum(jnp.transpose(gb[...]))
-            wait_plane, sent_plane = gather(
-                gram_sum, g1s, g1, plane_mate, PLANE_STEPS, plane_index, red_send.at[0], red_recv.at[0]
+            wait_plane = gather(
+                gram_sum, g1s, g1, plane_mate, PLANE_STEPS, plane_index, red_recv.at[0], True
             )
         wait_near()
 
@@ -483,17 +480,17 @@
         basis.append(2.0 * (ub[...] * dinv - SHIFTS[k] * basis[k]))
 
     last_sum = lane_sum(jnp.sum(basis[ITERS - 1] * ub[...], axis=0, keepdims=True))
-    wait_last_plane, sent_last_plane = gather(
-        last_sum, b1s, b1, plane_mate, PLANE_STEPS, plane_index, red_send.at[4], red_recv.at[4]
+    wait_last_plane = gather(
+        last_sum, b1s, b1, plane_mate, PLANE_STEPS, plane_index, red_recv.at[3], True
     )
     replicate(ITERS)
     wait_plane()
     plane_sum = pairs_of(g1, PLANE)
-    wait_tower, sent_tower = gather(plane_sum, g2s, g2, tower_mate, TOWER_STEPS, z, red_send.at[1], red_recv.at[1], g1)
+    wait_tower = gather(plane_sum, g2s, g2, tower_mate, TOWER_STEPS, z, red_recv.at[1], False)
     wait_last_plane()
     last_plane_sum = pairs_of(b1, PLANE)
-    wait_last_tower, sent_last_tower = gather(
-        last_plane_sum, b2s, b2, tower_mate, TOWER_STEPS, z, red_send.at[5], red_recv.at[5], b1
+    wait_last_tower = gather(
+        last_plane_sum, b2s, b2, tower_mate, TOWER_STEPS, z, red_recv.at[4], False
     )
     wait_tower()
     total = pairs_of(g2, ZLEN)
@@ -551,8 +548,7 @@
     drop = combine(image[0], ITERS + 1) * diag
     pressure = combine(solution_at[0], ITERS - 1)
     along = combine(direction[0], ITERS)
-    for k in range(ITERS + 1):
-        wait_replicas(k, row_recv)
+    wait_replicas(row_recv)
 
     def row_combine(factors, count, t):
         out = None
@@ -586,8 +582,8 @@
     gb[ITERS - 1 : ITERS, :] = jnp.max(peaks[ITERS - 1], axis=0, keepdims=True)
     peak = jnp.max(gb[0:8, :], axis=1, keepdims=True)
     peak_row = jnp.sum(jnp.where(sub8 == lane8, peak, 0.0), axis=0, keepdims=True)
-    wait_peaks, sent_peaks = gather(
-        [peak_row], p1s, p1, wall_mate, WALL_STEPS, y * ZLEN + z, red_send.at[2], red_recv.at[2], p1
+    wait_peaks = gather(
+        [peak_row], p1s, p1, wall_mate, WALL_STEPS, y * ZLEN + z, red_recv.at[2], False
     )
 
     density = rb[1, pl.ds(8, ROWS), :]
@@ -600,25 +596,29 @@
         copy = pltpu.make_async_remote_copy(
             src_ref=osb.at[pl.ds(2 * k, 2)],
             dst_ref=ob.at[place],
-            send_sem=out_send.at[k],
+            send_sem=out_send,
             recv_sem=out_recv,
             device_id=(k, group),
             device_id_type=MESH,
         )
         pl.when(wanted)(copy.start)
-        sends.append((wanted, copy))
     local = pltpu.make_async_copy(osb.at[pl.ds(2 * a, 2)], ob.at[place], out_recv)
     pl.when(group == q)(local.start)
 
     wait_peaks()
     pltpu.make_async_copy(ob, ob, out_recv).wait()
 
-    for wanted, copy in sends:
-        pl.when(wanted)(copy.wait_send)
-    for wait in (sent_plane, sent_tower, sent_last_plane, sent_last_tower, sent_peaks):
+    for wait in sends:
         wait()
-    for k in range(ITERS + 1):
-        wait_replicas(k, row_send)
+    wait_replicas(row_send)
+    for sem, kept, cell in ((in_send, sbuf, 1), (out_send, osb, 2)):
+        some, all_ = kept.at[pl.ds(0, (GX - 1) * cell)], kept.at[pl.ds(0, GX * cell)]
+        pl.when(home == q)(pltpu.make_async_copy(some, some, sem).wait)
+        pl.when(home != q)(pltpu.make_async_copy(all_, all_, sem).wait)
+    planes = part.at[0, pl.ds(0, 4 * len(PLANE_STEPS))]
+    total_sent = part.at[0:2, pl.ds(0, 2 * len(PLANE_STEPS) + 2 * len(TOWER_STEPS) + len(WALL_STEPS) // 2)]
+    pl.when(core == 0)(pltpu.make_async_copy(planes, planes, red_send).wait)
+    pl.when(core == 1)(pltpu.make_async_copy(total_sent, total_sent, red_send).wait)
 
 
 def finish(ob, p1, dens_ref, pres_ref, resid_ref, peaks_ref):
@@ -672,19 +672,19 @@
             pltpu.VMEM((ROWS, 4, SLOT), F32),
             pltpu.VMEM((ITERS + 1, 2 * XLEN, ROWS, SLOT), F32),
             dma((4,)),
-            dma((GX,)),
+            dma,
+            dma,
             dma,
             dma((2,)),
-            dma((3,)),
+            dma,
             dma((2,)),
-            dma((3,)),
+            dma((ITERS,)),
             dma((ITERS, 2)),
-            dma((ITERS, 3)),
-            dma((6,)),
-            dma((6,)),
-            dma((ITERS + 1,)),
-            dma((ITERS + 1,)),
-            dma((GX,)),
+            dma,
+            dma((5,)),
+            dma,
+            dma,
+            dma,
             dma,
         ],
         compiler_params=pltpu.CompilerParams(collective_id=0, has_side_effects=True),

time: 50.4 us -> 50 us (level)
  no operation moved by 1% of the time
where the time goes in v9:
time: 50 us; the launch traced here: 49.8 us
  Pallas kernels  49.1 us (98%)
  between operations  0.64 us (1%)
    pallas_call x1, Pallas kernels, shard(): pl.pallas_call(body, out_shape=(pltpu.VMEM((GX, 2, 4, SLOT), F32), pltpu....  48.5 us

profile of v9, /device:TPU:1, one launch (start us, length us, event | category | flops | bytes accessed | tf_op | source)
XLA Modules:
  0.0 49.8 jit_solution(13985714595992056978)
XLA Ops:
  0.6 48.5 %shard_map.75 = (f32[8,2,4,128]{3,2,1,0:T(4,128)S(1)}, f32[32,1,128]{2,1,0:T(1,128)S(1)}) custom-call(f32[2,2,8,128]{3,2,1,0:T(8,128)} %off_hbm.1, f32[2,8,128]{2,1,0:T(8,128)} %mass_hbm.1, s32[2,8]{1,0:T(2,128)} %cnt_hbm.1, f32[2,8,128]{2,1,0:T(8,128)} %src_hbm.1), custom_call_target="tpu_custom_call" | custom-call | tf_op jit(solution)/shard_map/pallas_call | solution.py:638
  49.1 0.6 %shard_map.76 = (f32[2,8,128]{2,1,0:T(8,128)}, f32[2,8,128]{2,1,0:T(8,128)}, f32[2,8,128]{2,1,0:T(8,128)}, f32[5]{0:T(128)}) custom-call(f32[8,2,4,128]{3,2,1,0:T(4,128)S(1)} %get-tuple-element.6.ob, f32[32,1,128]{2,1,0:T(1,128)S(1)} %get-tuple-element.7.p1), custom_call_target="tpu_custom_call" | custom-call | tf_op jit(solution)/shard_map/pallas_call | solution.py:692
